TPU v7x, 32 devices: a whole 2x2x4 slice. The times are simulated.
32 devices in a mesh: g: 32 (over z, y, x, core).
Axes of the slice: x: 2, y: 2, z: 4, core: 2. Of those that a mesh axis runs over, the one named last changes fastest.
Arguments:
- x: bfloat16 [16384, 4096], P(None, 'g')
- ws1: bfloat16 [4096, 256], P('g')
- wn1: bfloat16 [4096, 256], P('g')
- ws2: bfloat16 [256, 256], replicated
- wn2: bfloat16 [256, 256], replicated
- ws3: bfloat16 [256, 47], replicated
- wn3: bfloat16 [256, 47], replicated
- nbr: int32 [16384, 10], P('g')
- nmask: int32 [16384, 10], P('g')
- labels: int32 [16384], P('g')
Outputs:
- output 1: float32 [], replicated
- output 2: float32 [4096, 256], P('g')
- output 3: float32 [4096, 256], P('g')
- output 4: float32 [256, 256], replicated
- output 5: float32 [256, 256], replicated
- output 6: float32 [256, 47], replicated
- output 7: float32 [256, 47], replicated
All inputs are finite; a program needn't handle non-finite values.
Results may differ from a plain program's by a relative error of at most 0.0139848.
Values are sent between devices in bfloat16 or wider.
A program may use at most 1 GiB of HBM per device.

v0:
```python
import jax
import jax.numpy as jnp
from jax import lax
from jax.sharding import PartitionSpec as P


def _dot(a, b):
    return jnp.dot(a, b, preferred_element_type=jnp.float32)


def _tdot(a, b):
    return lax.dot_general(a, b, (((0,), (0,)), ((), ())), preferred_element_type=jnp.float32)


def _mean_nbr(y, nbr, nmask):
    acc = jnp.zeros((nbr.shape[0], y.shape[1]), jnp.float32)
    for k in range(nbr.shape[1]):
        acc = acc + jnp.where(nmask[:, k:k + 1] > 0, y[nbr[:, k]].astype(jnp.float32), 0.0)
    return acc / jnp.sum(nmask, axis=1, keepdims=True).astype(jnp.float32)


def _mean_nbr_t(g, nbr, nmask, rows):
    gs = g.astype(jnp.float32) / jnp.sum(nmask, axis=1, keepdims=True).astype(jnp.float32)
    acc = jnp.zeros((rows, g.shape[1]), jnp.float32)
    for k in range(nbr.shape[1]):
        acc = acc.at[nbr[:, k]].add(jnp.where(nmask[:, k:k + 1] > 0, gs, 0.0))
    return acc


def solution(mesh):
    def body(x, ws1, wn1, ws2, wn2, ws3, wn3, nbr, nmask, labels):
        bf = jnp.bfloat16
        nodes = x.shape[0]
        nbr_all = lax.all_gather(nbr, 'g', axis=0, tiled=True)
        mask_all = lax.all_gather(nmask, 'g', axis=0, tiled=True)
        z1_part = _dot(x, ws1) + _mean_nbr(_dot(x, wn1), nbr_all, mask_all)
        z1 = lax.psum_scatter(z1_part, 'g', scatter_dimension=0, tiled=True)
        h1 = jnp.maximum(z1, 0.0).astype(bf)
        m1 = _mean_nbr(lax.all_gather(h1, 'g', axis=0, tiled=True), nbr, nmask).astype(bf)
        z2 = _dot(h1, ws2) + _dot(m1, wn2)
        h2 = jnp.maximum(z2, 0.0).astype(bf)
        m2 = _mean_nbr(lax.all_gather(h2, 'g', axis=0, tiled=True), nbr, nmask).astype(bf)
        logits = _dot(h2, ws3) + _dot(m2, wn3)
        lse = jax.nn.logsumexp(logits, axis=1)
        picked = jnp.take_along_axis(logits, labels[:, None], axis=1)[:, 0]
        loss = lax.psum(jnp.sum(lse - picked), 'g') / nodes
        onehot = jax.nn.one_hot(labels, ws3.shape[1], dtype=jnp.float32)
        d3 = ((jax.nn.softmax(logits, axis=1) - onehot) / nodes).astype(bf)
        dws3 = lax.psum(_tdot(h2, d3), 'g')
        dwn3 = lax.psum(_tdot(m2, d3), 'g')
        back2 = lax.psum_scatter(_mean_nbr_t(_dot(d3, wn3.T), nbr, nmask, nodes), 'g', scatter_dimension=0, tiled=True)
        d2 = jnp.where(z2 > 0, _dot(d3, ws3.T) + back2, 0.0).astype(bf)
        dws2 = lax.psum(_tdot(h1, d2), 'g')
        dwn2 = lax.psum(_tdot(m1, d2), 'g')
        back1 = lax.psum_scatter(_mean_nbr_t(_dot(d2, wn2.T), nbr, nmask, nodes), 'g', scatter_dimension=0, tiled=True)
        d1 = jnp.where(z1 > 0, _dot(d2, ws2.T) + back1, 0.0).astype(bf)
        d1_all = lax.all_gather(d1, 'g', axis=0, tiled=True)
        b1 = _mean_nbr_t(d1_all, nbr_all, mask_all, nodes).astype(bf)
        return loss, _tdot(x, d1_all), _tdot(x, b1), dws2, dwn2, dws3, dwn3

    rows = P('g', None)
    in_specs = (P(None, 'g'), rows, rows, P(), P(), P(), P(), rows, rows, P('g'))
    out_specs = (P(), rows, rows, P(), P(), P(), P())
    return jax.shard_map(body, mesh=mesh, in_specs=in_specs, out_specs=out_specs, check_vma=False)
```

profile of v0, /device:TPU:0, one launch (start us, length us, event | category | flops | bytes accessed | tf_op | source)
XLA Modules:
  0.0 3180.9 jit_solution(726194814909357174)
XLA Ops:
  7.2 46.1 %all_gather.16 = s32[16384,10]{0,1:T(8,128)S(1)} all-gather(s32[512,10]{0,1:T(8,128)} %param.17), channel_id=1, replica_groups=mesh['g'=32] {'g'}, dimensions={0}, use_global_device_ids=true | all-gather | bytes 675840 | tf_op jit(solution)/shard_map/all_gather | solution.py:34
  65.1 67.5 %gather_fusion = f32[16384,256]{1,0:T(8,128)} fusion(f32[16384,256]{1,0:T(8,128)} %fusion.135, s32[16384]{0:T(1024)S(1)} %broadcast_clamp_fusion.9), kind=kCustom, calls=%fused_computation | custom fusion | bytes 33619968 | tf_op jit(solution)/shard_map/gather | solution.py:18
  132.6 67.4 %gather_fusion.1 = f32[16384,256]{1,0:T(8,128)} fusion(f32[16384,256]{1,0:T(8,128)} %fusion.135, s32[16384]{0:T(1024)S(1)} %broadcast_clamp_fusion.8), kind=kCustom, calls=%fused_computation.1 | custom fusion | bytes 33619968 | tf_op jit(solution)/shard_map/gather | solution.py:18
  200.0 67.5 %gather_fusion.2 = f32[16384,256]{1,0:T(8,128)} fusion(f32[16384,256]{1,0:T(8,128)} %fusion.135, s32[16384]{0:T(1024)S(1)} %broadcast_clamp_fusion.7), kind=kCustom, calls=%fused_computation.2 | custom fusion | bytes 33619968 | tf_op jit(solution)/shard_map/gather | solution.py:18
  267.5 67.5 %gather_fusion.3 = f32[16384,256]{1,0:T(8,128)} fusion(f32[16384,256]{1,0:T(8,128)} %fusion.135, s32[16384]{0:T(1024)S(1)} %broadcast_clamp_fusion.6), kind=kCustom, calls=%fused_computation.3 | custom fusion | bytes 33619968 | tf_op jit(solution)/shard_map/gather | solution.py:18
  335.0 67.5 %gather_fusion.4 = f32[16384,256]{1,0:T(8,128)} fusion(f32[16384,256]{1,0:T(8,128)} %fusion.135, s32[16384]{0:T(1024)S(1)} %broadcast_clamp_fusion.5), kind=kCustom, calls=%fused_computation.4 | custom fusion | bytes 33619968 | tf_op jit(solution)/shard_map/gather | solution.py:18
  402.5 67.4 %gather_fusion.5 = f32[16384,256]{1,0:T(8,128)} fusion(f32[16384,256]{1,0:T(8,128)} %fusion.135, s32[16384]{0:T(1024)S(1)} %broadcast_clamp_fusion.4), kind=kCustom, calls=%fused_computation.5 | custom fusion | bytes 33619968 | tf_op jit(solution)/shard_map/gather | solution.py:18
  470.0 67.5 %gather_fusion.6 = f32[16384,256]{1,0:T(8,128)} fusion(f32[16384,256]{1,0:T(8,128)} %fusion.135, s32[16384]{0:T(1024)S(1)} %broadcast_clamp_fusion.3), kind=kCustom, calls=%fused_computation.6 | custom fusion | bytes 33619968 | tf_op jit(solution)/shard_map/gather | solution.py:18
  537.5 67.5 %gather_fusion.7 = f32[16384,256]{1,0:T(8,128)} fusion(f32[16384,256]{1,0:T(8,128)} %fusion.135, s32[16384]{0:T(1024)S(1)} %broadcast_clamp_fusion.2), kind=kCustom, calls=%fused_computation.7 | custom fusion | bytes 33619968 | tf_op jit(solution)/shard_map/gather | solution.py:18
  605.0 67.5 %gather_fusion.8 = f32[16384,256]{1,0:T(8,128)} fusion(f32[16384,256]{1,0:T(8,128)} %fusion.135, s32[16384]{0:T(1024)S(1)} %broadcast_clamp_fusion.1), kind=kCustom, calls=%fused_computation.8 | custom fusion | bytes 33619968 | tf_op jit(solution)/shard_map/gather | solution.py:18
  672.5 67.5 %gather_fusion.9 = f32[16384,256]{1,0:T(8,128)} fusion(f32[16384,256]{1,0:T(8,128)} %fusion.135, s32[16384]{0:T(1024)S(1)} %broadcast_clamp_fusion), kind=kCustom, calls=%fused_computation.9 | custom fusion | bytes 33619968 | tf_op jit(solution)/shard_map/gather | solution.py:18
  740.0 39.5 %all_gather.15 = s32[16384,10]{0,1:T(8,128)S(1)} all-gather(s32[512,10]{0,1:T(8,128)S(1)} %copy-done.17), channel_id=1, replica_groups=mesh['g'=32] {'g'}, dimensions={0}, use_global_device_ids=true | all-gather | bytes 675840 | tf_op jit(solution)/shard_map/all_gather | solution.py:35
  781.8 57.3 %convolution_add_fusion = f32[16384,256]{1,0:T(8,128)} fusion(bf16[16384,128]{1,0:T(8,128)(2,1)} %param.10, bf16[128,256]{1,0:T(8,128)(2,1)S(1)} %copy-done.34, f32[16384,256]{1,0:T(8,128)} %gather_fusion.9, f32[16384,256]{1,0:T(8,128)} %gather_fusion.8, f32[16384,256]{1,0:T(8,128)} %gather_fusion.7, f32[16384,256]{1,0:T(8,128)} %gather_fusion.6, ...), kind=kOutput, calls=%fused_computation.61 | convolution fusion | flops 1161822208 | bytes 189038592 | tf_op jit(solution)/shard_map/dot_general | solution.py:8
  839.3 180.3 %reduce-scatter.4.cloned.1.call-done = f32[512,256]{1,0:T(8,128)} async-done(((f32[16384,256]{1,0:T(8,128)}), f32[512,256]{1,0:T(8,128)}) %reduce-scatter.4.cloned.1.call-update) | async-done | bytes 524304 | tf_op jit(solution)/shard_map/reduce_scatter | solution.py:37
  1023.7 77.9 %all-gather.4.cloned.1.call-done = bf16[16384,256]{1,0:T(8,128)(2,1)} async-done(((bf16[512,256]{1,0:T(8,128)(2,1)}), bf16[16384,256]{1,0:T(8,128)(2,1)}) %all-gather.4.cloned.1.call-update) | async-done | bytes 8388624 | tf_op jit(solution)/shard_map/all_gather | solution.py:39
  1168.1 74.6 %all-gather.6.cloned.1.call-done = bf16[16384,256]{1,0:T(8,128)(2,1)} async-done(((bf16[512,256]{1,0:T(8,128)(2,1)}), bf16[16384,256]{1,0:T(8,128)(2,1)}) %all-gather.6.cloned.1.call-update) | async-done | bytes 8388624 | tf_op jit(solution)/shard_map/all_gather | solution.py:42
  1319.0 14.9 scatter_custom_fusion.1
  1334.0 14.7 scatter_custom_fusion.2
  1348.7 14.7 scatter_custom_fusion.3
  1363.4 14.7 scatter_custom_fusion.4
  1378.2 15.1 scatter_custom_fusion.5
  1393.3 14.7 scatter_custom_fusion.6
  1408.1 14.7 scatter_custom_fusion.7
  1422.8 14.7 scatter_custom_fusion.8
  1437.5 14.7 scatter_custom_fusion.9
  1452.5 181.6 %reduce-scatter.6.cloned.1.call-done = f32[512,256]{1,0:T(8,128)} async-done(((f32[16384,256]{1,0:T(8,128)}), f32[512,256]{1,0:T(8,128)}) %reduce-scatter.6.cloned.1.call-update) | async-done | bytes 524304 | tf_op jit(solution)/shard_map/reduce_scatter | solution.py:51
  1646.1 14.7 scatter_custom_fusion.11
  1660.8 14.9 scatter_custom_fusion.12
  1675.7 14.7 scatter_custom_fusion.13
  1690.4 14.7 scatter_custom_fusion.14
  1705.2 14.7 scatter_custom_fusion.15
  1719.9 14.7 scatter_custom_fusion.16
  1734.6 15.1 scatter_custom_fusion.17
  1749.8 14.7 scatter_custom_fusion.18
  1764.5 14.8 scatter_custom_fusion.19
  1779.4 184.6 %reduce-scatter.8.cloned.1.call-done = f32[512,256]{1,0:T(8,128)} async-done(((f32[16384,256]{1,0:T(8,128)}), f32[512,256]{1,0:T(8,128)}) %reduce-scatter.8.cloned.1.call-update) | async-done | bytes 524304 | tf_op jit(solution)/shard_map/reduce_scatter | solution.py:55
  1971.7 44.4 %all-reduce.6 = (f32[]{:T(128)}, f32[256,47]{0,1:T(8,128)}, f32[256,47]{0,1:T(8,128)}) all-reduce(f32[]{:T(128)} %subtract_reduce_fusion, f32[256,47]{0,1:T(8,128)S(1)} %fusion.140, f32[256,47]{0,1:T(8,128)S(1)} %fusion.141), channel_id=1, replica_groups=mesh['g'=32] {'g'}, use_global_device_ids=true, to_apply=%region_6.7 | all-reduce | flops 24065 | bytes 192520 | tf_op jit(solution)/shard_map/psum | solution.py:46
  2018.7 26.8 all-gather.8.cloned.1.call-done
  2045.4 106.5 %scatter_custom_fusion.20 = f32[16384,256]{1,0:T(8,128)} fusion(s32[16384]{0:T(1024)} %bitcast.79, f32[]{:T(128)} %constant.10.clone.1, pred[16384]{0:T(1024)(128)(4,1)S(1)} %get-tuple-element.21, bf16[16384,256]{1,0:T(8,128)(2,1)} %all-gather.8.cloned.1.call-done, f32[16384]{0:T(1024)S(1)} %convert_element_type.111), kind=kCustom, calls=%fused_computation.83 | custom fusion | flops 16777216 | bytes 25248768 | tf_op jit(solution)/shard_map/scatter-add | solution.py:26
  2152.0 111.1 %scatter_custom_fusion.21 = f32[16384,256]{1,0:T(8,128)} fusion(f32[16384,256]{1,0:T(8,128)} %scatter_custom_fusion.20, s32[16384]{0:T(1024)} %bitcast.77, f32[]{:T(128)} %constant.10.clone.1, pred[16384]{0:T(1024)(128)(4,1)S(1)} %get-tuple-element.30, bf16[16384,256]{1,0:T(8,128)(2,1)} %all-gather.8.cloned.1.call-done, f32[16384]{0:T(1024)S(1)} %convert_element_type.111), kind=kCustom, calls=%fused_computation.78 | custom fusion | flops 16777216 | bytes 25248256 | tf_op jit(solution)/shard_map/scatter-add | solution.py:26
  2263.1 111.1 %scatter_custom_fusion.22 = f32[16384,256]{1,0:T(8,128)} fusion(f32[16384,256]{1,0:T(8,128)} %scatter_custom_fusion.21, s32[16384]{0:T(1024)} %bitcast.75, f32[]{:T(128)} %constant.10.clone.1, pred[16384]{0:T(1024)(128)(4,1)S(1)} %get-tuple-element.29, bf16[16384,256]{1,0:T(8,128)(2,1)} %all-gather.8.cloned.1.call-done, f32[16384]{0:T(1024)S(1)} %convert_element_type.111), kind=kCustom, calls=%fused_computation.76 | custom fusion | flops 16777216 | bytes 25248256 | tf_op jit(solution)/shard_map/scatter-add | solution.py:26
  2374.2 111.1 %scatter_custom_fusion.23 = f32[16384,256]{1,0:T(8,128)} fusion(f32[16384,256]{1,0:T(8,128)} %scatter_custom_fusion.22, s32[16384]{0:T(1024)} %bitcast.73, f32[]{:T(128)} %constant.10.clone.1, pred[16384]{0:T(1024)(128)(4,1)S(1)} %copy-done.31, bf16[16384,256]{1,0:T(8,128)(2,1)} %all-gather.8.cloned.1.call-done, f32[16384]{0:T(1024)S(1)} %convert_element_type.111), kind=kCustom, calls=%fused_computation.74 | custom fusion | flops 16777216 | bytes 25248256 | tf_op jit(solution)/shard_map/scatter-add | solution.py:26
  2485.3 111.3 %scatter_custom_fusion.24 = f32[16384,256]{1,0:T(8,128)} fusion(f32[16384,256]{1,0:T(8,128)} %scatter_custom_fusion.23, s32[16384]{0:T(1024)} %bitcast.71, f32[]{:T(128)} %constant.10.clone.1, pred[16384]{0:T(1024)(128)(4,1)S(1)} %copy-done.29, bf16[16384,256]{1,0:T(8,128)(2,1)} %all-gather.8.cloned.1.call-done, f32[16384]{0:T(1024)S(1)} %convert_element_type.111), kind=kCustom, calls=%fused_computation.72 | custom fusion | flops 16777216 | bytes 25248256 | tf_op jit(solution)/shard_map/scatter-add | solution.py:26
  2596.6 111.1 %scatter_custom_fusion.25 = f32[16384,256]{1,0:T(8,128)} fusion(f32[16384,256]{1,0:T(8,128)} %scatter_custom_fusion.24, s32[16384]{0:T(1024)} %bitcast.69, f32[]{:T(128)} %constant.10.clone.1, pred[16384]{0:T(1024)(128)(4,1)S(1)} %copy-done.27, bf16[16384,256]{1,0:T(8,128)(2,1)} %all-gather.8.cloned.1.call-done, f32[16384]{0:T(1024)S(1)} %convert_element_type.111), kind=kCustom, calls=%fused_computation.70 | custom fusion | flops 16777216 | bytes 25248256 | tf_op jit(solution)/shard_map/scatter-add | solution.py:26
  2707.7 111.1 %scatter_custom_fusion.26 = f32[16384,256]{1,0:T(8,128)} fusion(f32[16384,256]{1,0:T(8,128)} %scatter_custom_fusion.25, s32[16384]{0:T(1024)} %bitcast.67, f32[]{:T(128)} %constant.10.clone.1, pred[16384]{0:T(1024)(128)(4,1)S(1)} %copy-done.25, bf16[16384,256]{1,0:T(8,128)(2,1)} %all-gather.8.cloned.1.call-done, f32[16384]{0:T(1024)S(1)} %convert_element_type.111), kind=kCustom, calls=%fused_computation.68 | custom fusion | flops 16777216 | bytes 25248256 | tf_op jit(solution)/shard_map/scatter-add | solution.py:26
  2818.8 111.1 %scatter_custom_fusion.27 = f32[16384,256]{1,0:T(8,128)} fusion(f32[16384,256]{1,0:T(8,128)} %scatter_custom_fusion.26, s32[16384]{0:T(1024)} %bitcast.65, f32[]{:T(128)} %constant.10.clone.1, pred[16384]{0:T(1024)(128)(4,1)S(1)} %copy-done.23, bf16[16384,256]{1,0:T(8,128)(2,1)} %all-gather.8.cloned.1.call-done, f32[16384]{0:T(1024)S(1)} %convert_element_type.111), kind=kCustom, calls=%fused_computation.66 | custom fusion | flops 16777216 | bytes 25248256 | tf_op jit(solution)/shard_map/scatter-add | solution.py:26
  2929.9 111.3 %scatter_custom_fusion.28 = f32[16384,256]{1,0:T(8,128)} fusion(f32[16384,256]{1,0:T(8,128)} %scatter_custom_fusion.27, s32[16384]{0:T(1024)} %bitcast.63, f32[]{:T(128)} %constant.10.clone.1, pred[16384]{0:T(1024)(128)(4,1)S(1)} %copy-done.21, bf16[16384,256]{1,0:T(8,128)(2,1)} %all-gather.8.cloned.1.call-done, f32[16384]{0:T(1024)S(1)} %convert_element_type.111), kind=kCustom, calls=%fused_computation.64 | custom fusion | flops 16777216 | bytes 25248256 | tf_op jit(solution)/shard_map/scatter-add | solution.py:26
  3041.3 111.1 %scatter_custom_fusion.29 = f32[16384,256]{1,0:T(8,128)} fusion(f32[16384,256]{1,0:T(8,128)} %scatter_custom_fusion.28, s32[16384]{0:T(1024)} %bitcast.61, f32[]{:T(128)} %constant.10.clone.1, pred[16384]{0:T(1024)(128)(4,1)S(1)} %copy-done.19, bf16[16384,256]{1,0:T(8,128)(2,1)} %all-gather.8.cloned.1.call-done, f32[16384]{0:T(1024)S(1)} %convert_element_type.111), kind=kCustom, calls=%fused_computation.62 | custom fusion | flops 16777216 | bytes 25248256 | tf_op jit(solution)/shard_map/scatter-add | solution.py:26
  (248 shorter events, 202.1 us)
Async XLA Ops:
  7.2 1158.6 %copy-start = (bf16[256,256]{1,0:T(8,128)(2,1)S(1)}, bf16[256,256]{1,0:T(8,128)(2,1)}, u32[]{:S(2)}) copy-start(bf16[256,256]{1,0:T(8,128)(2,1)} %param.14) | copy-start | bytes 393220
  7.2 1012.4 %reduce-scatter.4.cloned.1.call-start = ((), (), s32[]{:S(2)}) async-start(), calls=%async_computation.3 | async-start | bytes 17301504 | tf_op jit(solution)/shard_map/reduce_scatter | solution.py:37
  54.2 145.8 %copy-start.14 = (s32[16384,1]{0,1:T(1,128)}, s32[16384,1]{0,1:T(1,128)S(1)}, u32[]{:S(2)}) copy-start(s32[16384,1]{0,1:T(1,128)S(1)} %get-tuple-element.56) | copy-start | bytes 196612
  54.2 213.3 %copy-start.13 = (s32[16384,1]{0,1:T(1,128)}, s32[16384,1]{0,1:T(1,128)S(1)}, u32[]{:S(2)}) copy-start(s32[16384,1]{0,1:T(1,128)S(1)} %get-tuple-element.55) | copy-start | bytes 196612
  54.2 280.8 %copy-start.12 = (s32[16384,1]{0,1:T(1,128)}, s32[16384,1]{0,1:T(1,128)S(1)}, u32[]{:S(2)}) copy-start(s32[16384,1]{0,1:T(1,128)S(1)} %get-tuple-element.54) | copy-start | bytes 196612
  54.2 348.3 %copy-start.11 = (s32[16384,1]{0,1:T(1,128)}, s32[16384,1]{0,1:T(1,128)S(1)}, u32[]{:S(2)}) copy-start(s32[16384,1]{0,1:T(1,128)S(1)} %get-tuple-element.53) | copy-start | bytes 196612
  54.2 415.7 %copy-start.10 = (s32[16384,1]{0,1:T(1,128)}, s32[16384,1]{0,1:T(1,128)S(1)}, u32[]{:S(2)}) copy-start(s32[16384,1]{0,1:T(1,128)S(1)} %get-tuple-element.52) | copy-start | bytes 196612
  54.3 483.2 %copy-start.9 = (s32[16384,1]{0,1:T(1,128)}, s32[16384,1]{0,1:T(1,128)S(1)}, u32[]{:S(2)}) copy-start(s32[16384,1]{0,1:T(1,128)S(1)} %get-tuple-element.51) | copy-start | bytes 196612
  54.3 550.7 %copy-start.8 = (s32[16384,1]{0,1:T(1,128)}, s32[16384,1]{0,1:T(1,128)S(1)}, u32[]{:S(2)}) copy-start(s32[16384,1]{0,1:T(1,128)S(1)} %get-tuple-element.50) | copy-start | bytes 196612
  54.3 618.2 %copy-start.7 = (s32[16384,1]{0,1:T(1,128)}, s32[16384,1]{0,1:T(1,128)S(1)}, u32[]{:S(2)}) copy-start(s32[16384,1]{0,1:T(1,128)S(1)} %get-tuple-element.49) | copy-start | bytes 196612
  839.2 182.3 %copy-start.33 = (s32[512,10]{0,1:T(8,128)S(1)}, s32[512,10]{0,1:T(8,128)}, u32[]{:S(2)}) copy-start(s32[512,10]{0,1:T(8,128)} %param.17) | copy-start | bytes 61444
  839.2 183.2 %copy-start.5 = (bf16[256,256]{1,0:T(8,128)(2,1)S(1)}, bf16[256,256]{1,0:T(8,128)(2,1)}, u32[]{:S(2)}) copy-start(bf16[256,256]{1,0:T(8,128)(2,1)} %param.13) | copy-start | bytes 393220
  839.2 327.7 %copy-start.32 = (bf16[256,47]{0,1:T(8,128)(2,1)S(1)}, bf16[256,47]{0,1:T(8,128)(2,1)}, u32[]{:S(2)}) copy-start(bf16[256,47]{0,1:T(8,128)(2,1)} %param.15) | copy-start | bytes 72196
  839.2 262.4 %all-gather.4.cloned.1.call-start = ((), (), s32[]{:S(2)}) async-start(), calls=%async_computation.4 | async-start | bytes 8650752 | tf_op jit(solution)/shard_map/all_gather | solution.py:39
  1021.4 221.3 %all-gather.6.cloned.1.call-start = ((), (), s32[]{:S(2)}) async-start(), calls=%async_computation.5 | async-start | bytes 8650752 | tf_op jit(solution)/shard_map/all_gather | solution.py:42
  1021.6 145.2 %copy-start.45 = (s32[1024]{0:T(1024)}, s32[1024]{0:T(1024)S(1)}, u32[]{:S(2)}) copy-start(s32[1024]{0:T(1024)S(1)} %pad_clamp_fusion.9) | copy-start | bytes 12292
  1022.1 128.4 %copy-start.44 = (s32[1024]{0:T(1024)}, s32[1024]{0:T(1024)S(1)}, u32[]{:S(2)}) copy-start(s32[1024]{0:T(1024)S(1)} %pad_clamp_fusion.8) | copy-start | bytes 12292
  1022.1 128.3 %copy-start.43 = (s32[1024]{0:T(1024)}, s32[1024]{0:T(1024)S(1)}, u32[]{:S(2)}) copy-start(s32[1024]{0:T(1024)S(1)} %pad_clamp_fusion.7) | copy-start | bytes 12292
  1022.1 128.3 %copy-start.42 = (s32[1024]{0:T(1024)}, s32[1024]{0:T(1024)S(1)}, u32[]{:S(2)}) copy-start(s32[1024]{0:T(1024)S(1)} %pad_clamp_fusion.6) | copy-start | bytes 12292
  1022.2 128.3 %copy-start.41 = (s32[1024]{0:T(1024)}, s32[1024]{0:T(1024)S(1)}, u32[]{:S(2)}) copy-start(s32[1024]{0:T(1024)S(1)} %pad_clamp_fusion.5) | copy-start | bytes 12292
  1022.2 128.3 %copy-start.40 = (s32[1024]{0:T(1024)}, s32[1024]{0:T(1024)S(1)}, u32[]{:S(2)}) copy-start(s32[1024]{0:T(1024)S(1)} %pad_clamp_fusion.4) | copy-start | bytes 12292
  1022.2 128.2 %copy-start.39 = (s32[1024]{0:T(1024)}, s32[1024]{0:T(1024)S(1)}, u32[]{:S(2)}) copy-start(s32[1024]{0:T(1024)S(1)} %pad_clamp_fusion.3) | copy-start | bytes 12292
  1022.2 128.2 %copy-start.37 = (s32[1024]{0:T(1024)}, s32[1024]{0:T(1024)S(1)}, u32[]{:S(2)}) copy-start(s32[1024]{0:T(1024)S(1)} %pad_clamp_fusion.2) | copy-start | bytes 12292
  1022.4 144.3 %copy-start.46 = (pred[512]{0:T(512)(128)(4,1)}, pred[512]{0:T(512)(128)(4,1)S(1)}, u32[]{:S(2)}) copy-start(pred[512]{0:T(512)(128)(4,1)S(1)} %get-tuple-element.42) | copy-start | bytes 1540
  1022.4 144.3 %copy-start.48 = (pred[512]{0:T(512)(128)(4,1)}, pred[512]{0:T(512)(128)(4,1)S(1)}, u32[]{:S(2)}) copy-start(pred[512]{0:T(512)(128)(4,1)S(1)} %get-tuple-element.34) | copy-start | bytes 1540
  1022.4 144.3 %copy-start.50 = (pred[512]{0:T(512)(128)(4,1)}, pred[512]{0:T(512)(128)(4,1)S(1)}, u32[]{:S(2)}) copy-start(pred[512]{0:T(512)(128)(4,1)S(1)} %get-tuple-element.35) | copy-start | bytes 1540
  1022.5 144.3 %copy-start.52 = (pred[512]{0:T(512)(128)(4,1)}, pred[512]{0:T(512)(128)(4,1)S(1)}, u32[]{:S(2)}) copy-start(pred[512]{0:T(512)(128)(4,1)S(1)} %get-tuple-element.36) | copy-start | bytes 1540
  1022.5 144.3 %copy-start.54 = (pred[512]{0:T(512)(128)(4,1)}, pred[512]{0:T(512)(128)(4,1)S(1)}, u32[]{:S(2)}) copy-start(pred[512]{0:T(512)(128)(4,1)S(1)} %get-tuple-element.37) | copy-start | bytes 1540
  1022.5 144.3 %copy-start.56 = (pred[512]{0:T(512)(128)(4,1)}, pred[512]{0:T(512)(128)(4,1)S(1)}, u32[]{:S(2)}) copy-start(pred[512]{0:T(512)(128)(4,1)S(1)} %get-tuple-element.38) | copy-start | bytes 1540
  1022.5 144.3 %copy-start.58 = (pred[512]{0:T(512)(128)(4,1)}, pred[512]{0:T(512)(128)(4,1)S(1)}, u32[]{:S(2)}) copy-start(pred[512]{0:T(512)(128)(4,1)S(1)} %get-tuple-element.39) | copy-start | bytes 1540
  1022.5 144.3 %copy-start.60 = (pred[512]{0:T(512)(128)(4,1)}, pred[512]{0:T(512)(128)(4,1)S(1)}, u32[]{:S(2)}) copy-start(pred[512]{0:T(512)(128)(4,1)S(1)} %get-tuple-element.40) | copy-start | bytes 1540
  1022.5 144.3 %copy-start.62 = (pred[512]{0:T(512)(128)(4,1)}, pred[512]{0:T(512)(128)(4,1)S(1)}, u32[]{:S(2)}) copy-start(pred[512]{0:T(512)(128)(4,1)S(1)} %get-tuple-element.41) | copy-start | bytes 1540
  1022.5 144.3 %copy-start.64 = (pred[512]{0:T(512)(128)(4,1)}, pred[512]{0:T(512)(128)(4,1)S(1)}, u32[]{:S(2)}) copy-start(pred[512]{0:T(512)(128)(4,1)S(1)} %get-tuple-element.33) | copy-start | bytes 1540
  1156.5 151.6 %copy-start.35 = (bf16[256,47]{0,1:T(8,128)(2,1)S(1)}, bf16[256,47]{0,1:T(8,128)(2,1)}, u32[]{:S(2)}) copy-start(bf16[256,47]{0,1:T(8,128)(2,1)} %param.16) | copy-start | bytes 72196
  1156.5 151.9 %copy-start.36 = (s32[512]{0:T(512)S(1)}, s32[512]{0:T(512)}, u32[]{:S(2)}) copy-start(s32[512]{0:T(512)} %param.19) | copy-start | bytes 6148
  1165.8 120.1 %copy-start.38 = (s32[1024]{0:T(1024)S(1)}, s32[1024]{0:T(1024)}, u32[]{:S(2)}) copy-start(s32[1024]{0:T(1024)} %copy-done.37) | copy-start | bytes 12292
  1166.9 467.3 %reduce-scatter.6.cloned.1.call-start = ((), (), s32[]{:S(2)}) async-start(), calls=%async_computation.6 | async-start | bytes 17301504 | tf_op jit(solution)/shard_map/reduce_scatter | solution.py:51
  1437.5 198.2 %copy-start.65 = (pred[512]{0:T(512)(128)(4,1)S(1)}, pred[512]{0:T(512)(128)(4,1)}, u32[]{:S(2)}) copy-start(pred[512]{0:T(512)(128)(4,1)} %copy-done.64) | copy-start | bytes 1540
  1452.3 193.8 %copy-start.63 = (pred[512]{0:T(512)(128)(4,1)S(1)}, pred[512]{0:T(512)(128)(4,1)}, u32[]{:S(2)}) copy-start(pred[512]{0:T(512)(128)(4,1)} %copy-done.62) | copy-start | bytes 1540
  1452.3 511.7 %reduce-scatter.8.cloned.1.call-start = ((), (), s32[]{:S(2)}) async-start(), calls=%async_computation.7 | async-start | bytes 17301504 | tf_op jit(solution)/shard_map/reduce_scatter | solution.py:55
  1764.5 199.5 %copy-start.4 = (f32[512,256]{1,0:T(8,128)S(1)}, f32[512,256]{1,0:T(8,128)}, u32[]{:S(2)}) copy-start(f32[512,256]{1,0:T(8,128)} %reduce-scatter.4.cloned.1.call-done) | copy-start | bytes 1572868
  1764.5 199.5 %copy-start.6 = (bf16[256,256]{1,0:T(8,128)(2,1)S(1)}, bf16[256,256]{1,0:T(8,128)(2,1)}, u32[]{:S(2)}) copy-start(bf16[256,256]{1,0:T(8,128)(2,1)} %param.13) | copy-start | bytes 393220
  1764.5 206.4 %copy-start.3 = (bf16[512,256]{1,0:T(8,128)(2,1)S(1)}, bf16[512,256]{1,0:T(8,128)(2,1)}, u32[]{:S(2)}) copy-start(bf16[512,256]{1,0:T(8,128)(2,1)} %get-tuple-element.68) | copy-start | bytes 786436
  1764.5 253.2 %copy-start.2 = (bf16[512,256]{1,0:T(8,128)(2,1)S(1)}, bf16[512,256]{1,0:T(8,128)(2,1)}, u32[]{:S(2)}) copy-start(bf16[512,256]{1,0:T(8,128)(2,1)} %maximum_convert_fusion.1) | copy-start | bytes 786436
  1779.4 266.1 %all-gather.8.cloned.1.call-start = ((), (), s32[]{:S(2)}) async-start(), calls=%async_computation.8 | async-start | bytes 8650752 | tf_op jit(solution)/shard_map/all_gather | solution.py:57
  1966.1 1203.1 %all-reduce.5.cloned.1.call-start = ((), (), s32[]{:S(2)}) async-start(), calls=%async_computation.9 | async-start | bytes 1048576 | tf_op jit(solution)/shard_map/psum | solution.py:53
  2485.3 111.3 %copy-start.27 = (pred[16384]{0:T(1024)(128)(4,1)S(1)}, pred[16384]{0:T(1024)(128)(4,1)}, u32[]{:S(2)}) copy-start(pred[16384]{0:T(1024)(128)(4,1)} %copy-done.26) | copy-start | bytes 49156
  2929.9 111.3 %copy-start.19 = (pred[16384]{0:T(1024)(128)(4,1)S(1)}, pred[16384]{0:T(1024)(128)(4,1)}, u32[]{:S(2)}) copy-start(pred[16384]{0:T(1024)(128)(4,1)} %copy-done.18) | copy-start | bytes 49156
  (35 other events, 1385.4 us)
Sparse Core Ops, SparseCore 0:
  839.3 180.1 reduce-scatter.3
  1023.0 78.5 all-gather.3
  1166.9 75.7 all-gather.5
  1452.4 181.6 reduce-scatter.5
  1779.5 184.4 reduce-scatter.7
  1966.7 78.6 all-gather.7
  2051.5 128.2 all-reduce.4
where the time goes:
time: 3200 us; the launch traced here: 3180 us
  other arithmetic  1410 us (44%)
  local copies, waits for them, and re-layouts  810 us (25%)
  waiting for transfers between devices  726 us (23%)
  blocking collectives  130 us (4%)
  matrix products  92.3 us (3%)
    scatter-add x30, other arithmetic, _mean_nbr_t(): acc = acc.at[nbr[:, k]].add(jnp.where(nmask[:, k:k + 1] > 0, gs, 0.0))  1390 us
    gather x30, local copies, waits for them, and re-layouts, _mean_nbr(): y[nbr[:, k]].astype(jnp.float32)  799 us
    reduce_scatter x1, waiting for transfers between devices, body(): lax.psum_scatter(_mean_nbr_t(_dot(d2, wn2.T), nbr, nmask, nodes), 'g', sc...  185 us
    reduce_scatter x1, waiting for transfers between devices, body(): lax.psum_scatter(_mean_nbr_t(_dot(d3, wn3.T), nbr, nmask, nodes), 'g', sc...  182 us
    reduce_scatter x1, waiting for transfers between devices, body(): z1 = lax.psum_scatter(z1_part, 'g', scatter_dimension=0, tiled=True)  180 us
    all_gather x1, waiting for transfers between devices, body(): lax.all_gather(h1, 'g', axis=0, tiled=True)  77.9 us
    dot_general x10, matrix products, _dot(): return jnp.dot(a, b, preferred_element_type=jnp.float32)  74.8 us
    all_gather x1, waiting for transfers between devices, body(): lax.all_gather(h2, 'g', axis=0, tiled=True)  74.6 us
  transfers between devices with their start and end apart: 7, of which 6 were waited for; matrix products, arithmetic and copies ran while one was open for 36% of the time, Pallas kernels for 0%

commit v1 on v0

v1 whole, which is shorter than its diff:
```python
import jax
import jax.numpy as jnp
from jax import lax
from jax.experimental import pallas as pl
from jax.experimental.pallas import tpu as pltpu
from jax.sharding import PartitionSpec as P

BF = jnp.bfloat16
F32 = jnp.float32
MESH = pl.DeviceIdType.MESH


def _dot(a, b):
    return jnp.dot(a, b, preferred_element_type=F32)


def _dot_nt(a, b):
    return lax.dot_general(a, b, (((1,), (1,)), ((), ())), preferred_element_type=F32)


def _tdot(a, b):
    return lax.dot_general(a, b, (((0,), (0,)), ((), ())), preferred_element_type=F32)


def _split3(y):
    hi = y.astype(BF)
    rest = y - hi.astype(F32)
    mid = rest.astype(BF)
    low = (rest - mid.astype(F32)).astype(BF)
    return jnp.concatenate([hi, mid, low], axis=1)


def _sum3(y):
    c = y.shape[1] // 3
    return (y[:, 2 * c:] + y[:, c:2 * c]) + y[:, :c]


def _meet(peers):
    bar = pltpu.get_barrier_semaphore()
    for t in peers:
        pl.semaphore_signal(bar, inc=1, device_id=(t,), device_id_type=MESH)
    pl.semaphore_wait(bar, len(peers))


def _send(src, dst, ssem, rsem, to):
    return pltpu.make_async_remote_copy(
        src_ref=src, dst_ref=dst, send_sem=ssem, recv_sem=rsem, device_id=(to,), device_id_type=MESH)


def _layers(n, rows, classes, nodes,
            sn, a, bt, cnt, cntx, lab, ws2, wn2, ws3, wn3,
            db, dw2, dw3, loss,
            nx, h1x, h2x, d3x, d2x, d1x, ssem, rsem):
    me = lax.axis_index('g')
    hid = ws2.shape[0]
    lo, own, hi = pl.ds(0, rows), pl.ds(rows, rows), pl.ds(2 * rows, rows)
    has_lo, has_hi = me > 0, me < n - 1
    bar = pltpu.get_barrier_semaphore()

    def copies(buf, e):
        return (_send(buf.at[own], buf.at[hi], ssem.at[e, 0], rsem.at[e, 0], me - 1),
                _send(buf.at[own], buf.at[lo], ssem.at[e, 1], rsem.at[e, 1], me + 1))

    def start(buf, e):
        down, up = copies(buf, e)

        @pl.when(has_lo)
        def _():
            down.start()

        @pl.when(has_hi)
        def _():
            up.start()

    def arrive(buf, e):
        down, up = copies(buf, e)

        @pl.when(has_hi)
        def _():
            down.wait_recv()

        @pl.when(has_lo)
        def _():
            up.wait_recv()

    bufs = (nx, h1x, h2x, d3x, d2x, d1x)

    @pl.when(has_lo)
    def _():
        pl.semaphore_signal(bar, inc=1, device_id=(me - 1,), device_id_type=MESH)

    @pl.when(has_hi)
    def _():
        pl.semaphore_signal(bar, inc=1, device_id=(me + 1,), device_id_type=MESH)

    @pl.when(jnp.logical_not(has_lo))
    def _():
        for b in bufs:
            b[lo] = jnp.zeros((rows, b.shape[1]), b.dtype)

    @pl.when(jnp.logical_not(has_hi))
    def _():
        for b in bufs:
            b[hi] = jnp.zeros((rows, b.shape[1]), b.dtype)

    nx[own] = sn[:, hid:]

    pl.semaphore_wait(bar, has_lo.astype(jnp.int32) + has_hi.astype(jnp.int32))
    start(nx, 0)
    count = cnt[...]
    countx = cntx[...]
    acc = _sum3(_dot(a[:, rows:2 * rows], _split3(nx[own])))
    arrive(nx, 0)
    acc = acc + _sum3(_dot(a[:, :rows], _split3(nx[lo]))) + _sum3(_dot(a[:, 2 * rows:], _split3(nx[hi])))
    z1 = sn[:, :hid] + acc / count
    h1 = jnp.maximum(z1, 0.0).astype(BF)
    h1x[own] = h1
    start(h1x, 1)
    z2 = _dot(h1, ws2[...])
    arrive(h1x, 1)
    m1 = (_dot(a[...], h1x[...]) / count).astype(BF)
    z2 = z2 + _dot(m1, wn2[...])
    h2 = jnp.maximum(z2, 0.0).astype(BF)
    h2x[own] = h2
    start(h2x, 2)
    logits = _dot(h2, ws3[...])
    arrive(h2x, 2)
    m2 = (_dot(a[...], h2x[...]) / count).astype(BF)
    logits = logits + _dot(m2, wn3[...])
    cls = lax.broadcasted_iota(jnp.int32, logits.shape, 1)
    real = cls < classes
    top = jnp.max(jnp.where(real, logits, -jnp.inf), axis=1, keepdims=True)
    ex = jnp.where(real, jnp.exp(logits - top), 0.0)
    tot = jnp.sum(ex, axis=1, keepdims=True)
    hot = cls == lab[...]
    picked = jnp.sum(jnp.where(hot, logits, 0.0), axis=1, keepdims=True)
    loss[...] = jnp.broadcast_to(jnp.sum(jnp.log(tot) + top - picked, axis=0, keepdims=True) / nodes, loss.shape)
    d3 = ((ex / tot - hot.astype(F32)) / nodes).astype(BF)
    d3x[own] = d3
    start(d3x, 3)
    dw3[:, :hid] = _tdot(d3, h2)
    dw3[:, hid:] = _tdot(d3, m2)
    d2 = _dot_nt(d3, ws3[...])
    arrive(d3x, 3)
    d2 = d2 + _sum3(_dot(bt[...], _split3(_dot_nt(d3x[...], wn3[...]) / countx)))
    d2 = jnp.where(z2 > 0, d2, 0.0).astype(BF)
    d2x[own] = d2
    start(d2x, 4)
    dw2[:, :hid] = _tdot(h1, d2)
    dw2[:, hid:] = _tdot(m1, d2)
    d1 = _dot_nt(d2, ws2[...])
    arrive(d2x, 4)
    d1 = d1 + _sum3(_dot(bt[...], _split3(_dot_nt(d2x[...], wn2[...]) / countx)))
    d1 = jnp.where(z1 > 0, d1, 0.0).astype(BF)
    d1x[own] = d1
    start(d1x, 5)
    db[:, :hid] = d1
    arrive(d1x, 5)
    db[:, hid:] = _sum3(_dot(bt[...], _split3(d1x[...].astype(F32) / countx))).astype(BF)
    for e, b in enumerate(bufs):
        down, up = copies(b, e)

        @pl.when(has_lo)
        def _():
            down.wait_send()

        @pl.when(has_hi)
        def _():
            up.wait_send()


def _reduce(p, s, out, sout,
            mine, rc, rl, rr, rl2, rr2, rz, sa, s1, s2, s3, s4, g,
            lsem, c_s, c_r, x1_s, x1_r, y1_s, y1_r, x2_s, x2_r, y2_s, y2_r, z_s, z_r, q_s, q_r, t_s, t_r, u_s, u_r):
    me = lax.axis_index('g')
    c, x, y, z = me % 2, (me // 2) % 2, (me // 4) % 2, me // 8
    half = out.shape[1] // 2
    left, right = pl.ds(0, half), pl.ds(half, half)
    oc, ox, oy = me + 1 - 2 * c, me + 2 - 4 * x, me + 4 - 8 * y
    zs = [(z + 1 + i) % 4 for i in range(4)]
    oz = [q * 8 + me % 8 for q in zs]
    _meet([oc, ox, oy] + oz[:3])
    done = []

    def go(cp):
        cp.start()
        done.append(cp)
        return cp

    def small(i, src, dst, to):
        return go(_send(src, dst, q_s.at[i], q_r.at[i], to))

    sl = pltpu.make_async_copy(s.at[:, :, :, c], sa, lsem.at[4])
    sl.start()
    k1 = small(0, s.at[:, :, :, 1 - c], s1, oc)
    loads, cores = [], []
    for i in range(4):
        q = zs[i]
        ld = pltpu.make_async_copy(p.at[q, :, :, c], mine.at[q], lsem.at[i])
        ld.start()
        loads.append(ld)
        cores.append(go(_send(p.at[q, :, :, 1 - c], rc.at[q], c_s.at[i], c_r.at[i], oc)))
    first, second = [], []

    def step1(i):
        q = zs[i]
        loads[i].wait()
        cores[i].wait_recv()
        mine[q] = mine[q] + rc[q]
        first.append((
            go(_send(mine.at[q, :, 1 - x, :, left], rl.at[q], x1_s.at[i], x1_r.at[i], ox)),
            go(_send(mine.at[q, 1 - y, :, :, right], rr.at[q], y1_s.at[i], y1_r.at[i], oy))))

    def step2(i):
        q = zs[i]
        for cp in first[i]:
            cp.wait_recv()
        mine[q, :, x, :, left] = mine[q, :, x, :, left] + rl[q]
        mine[q, y, :, :, right] = mine[q, y, :, :, right] + rr[q]
        second.append((
            go(_send(mine.at[q, 1 - y, x, :, left], rl2.at[q], y2_s.at[i], y2_r.at[i], oy)),
            go(_send(mine.at[q, y, 1 - x, :, right], rr2.at[q], x2_s.at[i], x2_r.at[i], ox))))

    def step3(i):
        q = zs[i]
        for cp in second[i]:
            cp.wait_recv()
        mine[q, y, x, :, left] = mine[q, y, x, :, left] + rl2[q]
        mine[q, y, x, :, right] = mine[q, y, x, :, right] + rr2[q]
        if i < 3:
            return go(_send(mine.at[q, y, x], rz.at[i], z_s.at[i], z_r.at[i], oz[i]))

    step1(0)
    sl.wait()
    k1.wait_recv()
    sa[...] = sa[...] + s1[...]
    k2 = small(1, sa.at[:, :, 1 - x], s2, ox)
    step1(1)
    k2.wait_recv()
    sa[:, :, x] = sa[:, :, x] + s2[...]
    k3 = small(2, sa.at[:, 1 - y, x], s3, oy)
    step2(0)
    step1(2)
    k3.wait_recv()
    sa[:, y, x] = sa[:, y, x] + s3[...]
    k4 = [go(_send(sa.at[zs[i], y, x], s4.at[i], t_s.at[i], t_r.at[i], oz[i])) for i in range(3)]
    step2(1)
    fz = [step3(0)]
    step1(3)
    for cp in k4:
        cp.wait_recv()
    g[z, y, x, c] = ((sa[z, y, x] + s4[0]) + s4[1]) + s4[2]
    k5 = [go(_send(g.at[z, y, x, c], g.at[z, y, x, c], u_s.at[i], u_r.at[i], oz[i])) for i in range(3)]
    step2(2)
    fz.append(step3(1))
    for cp in k5:
        cp.wait_recv()
    k6 = small(3, g.at[:, y, x, c], g.at[:, y, x, c], oy)
    step2(3)
    k6.wait_recv()
    k7 = small(4, g.at[:, :, x, c], g.at[:, :, x, c], ox)
    fz.append(step3(2))
    k7.wait_recv()
    k8 = small(5, g.at[:, :, :, c], g.at[:, :, :, c], oc)
    step3(3)
    k8.wait_recv()
    sout[...] = g[...]
    for cp in fz:
        cp.wait_recv()
    out[...] = ((mine[z, y, x] + rz[0]) + rz[1]) + rz[2]
    for cp in done:
        cp.wait_send()


def solution(mesh):
    n = mesh.shape['g']
    up = [(i, i + 1) for i in range(n - 1)]
    down = [(i + 1, i) for i in range(n - 1)]
    vm = pl.BlockSpec(memory_space=pltpu.VMEM)
    hbm = pl.BlockSpec(memory_space=pl.ANY)
    dma = pltpu.SemaphoreType.DMA

    def ext(y):
        return jnp.concatenate([lax.ppermute(y, 'g', up), y, lax.ppermute(y, 'g', down)], axis=0)

    def body(x, ws1, wn1, ws2, wn2, ws3, wn3, nbr, nmask, labels):
        nodes = x.shape[0]
        rows, slots = nbr.shape
        hid = ws2.shape[0]
        classes = ws3.shape[1]
        feats = ws1.shape[0]
        pad = 128 - classes
        base = lax.axis_index('g') * rows
        xr = lax.all_to_all(x, 'g', 0, 1, tiled=True)
        w1 = lax.all_gather(jnp.concatenate([ws1, wn1], axis=1), 'g', axis=0, tiled=True)
        cnt = jnp.sum(nmask, axis=1, keepdims=True).astype(F32)
        col = jnp.where(nmask > 0, nbr - base + rows, -1)
        iota = lax.broadcasted_iota(jnp.int32, (rows, 3 * rows), 1)
        a = sum((col[:, k:k + 1] == iota).astype(F32) for k in range(slots)).astype(BF)
        ge = ext(jnp.concatenate([jnp.where(nmask > 0, nbr, -1), jnp.sum(nmask, axis=1, keepdims=True)], axis=1))
        cnt_e = jnp.maximum(ge[:, slots:], 1).astype(F32)
        col_e = jnp.where(cnt_e > 0, ge[:, :slots] - base, -1).T
        iota_e = lax.broadcasted_iota(jnp.int32, (rows, 3 * rows), 0)
        bt = sum((col_e[k:k + 1] == iota_e).astype(F32) for k in range(slots)).astype(BF)

        sn = _dot(xr, w1)
        wide = [(0, 0), (0, pad)]
        sds = jax.ShapeDtypeStruct
        db, dw2, dw3, loss = pl.pallas_call(
            lambda *r: _layers(n, rows, classes, nodes, *r),
            out_shape=(sds((rows, 2 * hid), BF), sds((hid, 2 * hid), F32), sds((128, 2 * hid), F32), sds((8, 128), F32)),
            in_specs=[vm] * 10, out_specs=(vm,) * 4,
            scratch_shapes=[pltpu.VMEM((3 * rows, hid), F32)] + [pltpu.VMEM((3 * rows, hid), BF)] * 2
            + [pltpu.VMEM((3 * rows, 128), BF)] + [pltpu.VMEM((3 * rows, hid), BF)] * 2 + [dma((6, 2)), dma((6, 2))],
            compiler_params=pltpu.CompilerParams(collective_id=1, has_side_effects=True, vmem_limit_bytes=56 << 20),
            name='layers',
        )(sn, a, bt, cnt, cnt_e, labels[:, None], ws2, wn2, jnp.pad(ws3, wide), jnp.pad(wn3, wide))

        dw1 = _tdot(xr, db)
        head = jnp.concatenate([dw3[:classes], jnp.broadcast_to(loss[:1, :1], (1, 2 * hid))], axis=0)
        small = jnp.concatenate([dw2, head], axis=0)
        small = jnp.concatenate([small[:, 128 * i:128 * (i + 1)] for i in range(2 * hid // 128)], axis=0)
        per = -(-small.shape[0] // n)
        per = -(-per // 8) * 8
        used = small.shape[0]
        small = jnp.pad(small, [(0, n * per - used), (0, 0)])
        own = feats
        grid = (4, 2, 2, 2)
        dw1, small = pl.pallas_call(
            _reduce,
            out_shape=(sds((own, 2 * hid), F32), sds(grid + (per, 128), F32)),
            in_specs=[hbm, hbm], out_specs=(vm, vm),
            scratch_shapes=[
                pltpu.VMEM((4, 2, 2, own, 2 * hid), F32), pltpu.VMEM((4, 2, 2, own, 2 * hid), F32),
                pltpu.VMEM((4, 2, own, hid), F32), pltpu.VMEM((4, 2, own, hid), F32),
                pltpu.VMEM((4, own, hid), F32), pltpu.VMEM((4, own, hid), F32),
                pltpu.VMEM((3, own, 2 * hid), F32),
                pltpu.VMEM((4, 2, 2, per, 128), F32), pltpu.VMEM((4, 2, 2, per, 128), F32),
                pltpu.VMEM((4, 2, per, 128), F32), pltpu.VMEM((4, per, 128), F32), pltpu.VMEM((3, per, 128), F32),
                pltpu.VMEM(grid + (per, 128), F32),
                dma((5,))] + [dma((4,))] * 10 + [dma((3,))] * 2 + [dma((6,))] * 2 + [dma((3,))] * 4,
            compiler_params=pltpu.CompilerParams(collective_id=2, has_side_effects=True, vmem_limit_bytes=56 << 20),
            name='reduce',
        )(dw1.reshape(grid + (own, 2 * hid)), small.reshape(grid + (per, 128)))
        small = small.reshape(n * per, 128)[:used]
        cut = used // (2 * hid // 128)
        small = jnp.concatenate([small[cut * i:cut * (i + 1)] for i in range(2 * hid // 128)], axis=1)
        head = small[hid:hid + classes]
        return (small[hid + classes, 0], dw1[:, :hid], dw1[:, hid:], small[:hid, :hid], small[:hid, hid:],
                head[:, :hid].T, head[:, hid:].T)

    r = P('g', None)
    in_specs = (P(None, 'g'), r, r, P(), P(), P(), P(), r, r, P('g'))
    out_specs = (P(), r, r, P(), P(), P(), P())
    return jax.shard_map(body, mesh=mesh, in_specs=in_specs, out_specs=out_specs, check_vma=False)
```

time: 3200 us -> 289 us (0.09)
  other arithmetic: 1410 us -> 15.8 us
  local copies, waits for them, and re-layouts: 810 us -> 25.2 us
  waiting for transfers between devices: 726 us -> 92 us
  blocking collectives: 130 us -> 0 us
  Pallas kernels: 0 us -> 116 us
  matrix products: 92.3 us -> 13.6 us
    scatter-add x30 -> x0, other arithmetic: 1390 us -> none  [_mean_nbr_t(): acc = acc.at[nbr[:, k]].add(jnp.where(nmask[:, k:k + 1] > 0, gs, 0.0))]
    gather x31 -> x0, local copies, waits for them, and re-layouts: 803 us -> none  [the longest x30 799 us: _mean_nbr(): y[nbr[:, k]].astype(jnp.float32)]
    reduce_scatter x3 -> x0, waiting for transfers between devices: 547 us -> none  [the longest x1 185 us: body(): lax.psum_scatter(_mean_nbr_t(_dot(d2, wn2.T), nbr, nmask, nodes), 'g', sc...]
    all_gather x3 -> x1, waiting for transfers between devices: 179 us -> 0.01 us  [body(): lax.all_gather(jnp.concatenate([ws1, wn1], axis=1), 'g', axis=0, tiled=True)]
    pallas_call x0 -> x2, Pallas kernels: none -> 116 us  [the longest x1 60.3 us: body(): pl.pallas_call(_reduce, out_shape=(sds((own, 2 * hid), F32), sds(grid + (...]
    all_to_all x0 -> x1, waiting for transfers between devices: none -> 92 us  [body(): xr = lax.all_to_all(x, 'g', 0, 1, tiled=True)]
    all_gather x2 -> x0, blocking collectives: 85.6 us -> none  [the longest x1 46.1 us: body(): nbr_all = lax.all_gather(nbr, 'g', axis=0, tiled=True)]
    dot_general x16 -> x2, matrix products: 92.3 us -> 13.6 us  [the longest x1 6.91 us: _dot(): return jnp.dot(a, b, preferred_element_type=F32)]
  transfers between devices with their start and end apart: 7 -> 4, of which waited for: 6 -> 1; matrix products, arithmetic and copies ran while one was open for 36% -> 8% of each run, Pallas kernels for 0% -> 0%
where the time goes in v1:
time: 289 us
  Pallas kernels  116 us (40%)
  waiting for transfers between devices  92 us (32%)
  local copies, waits for them, and re-layouts  25.2 us (9%)
  other arithmetic  15.8 us (5%)
  between operations  14.3 us (5%)
  matrix products  13.6 us (5%)
  starting transfers between devices  11.9 us (4%)
    all_to_all x1, waiting for transfers between devices, body(): xr = lax.all_to_all(x, 'g', 0, 1, tiled=True)  92 us
    pallas_call x1, Pallas kernels, body(): pl.pallas_call(_reduce, out_shape=(sds((own, 2 * hid), F32), sds(grid + (...  60.3 us
    pallas_call x1, Pallas kernels, body(): pl.pallas_call(lambda *r: _layers(n, rows, classes, nodes, *r), out_shape...  55.7 us
    dot_general x1, local copies, waits for them, and re-layouts, _tdot(): lax.dot_general(a, b, (((0,), (0,)), ((), ())), preferred_element_type=F32)  9 us
    all_to_all x1, starting transfers between devices, body(): xr = lax.all_to_all(x, 'g', 0, 1, tiled=True)  7.49 us
    dot_general x1, matrix products, _dot(): return jnp.dot(a, b, preferred_element_type=F32)  6.91 us
    dot_general x1, matrix products, _tdot(): lax.dot_general(a, b, (((0,), (0,)), ((), ())), preferred_element_type=F32)  6.66 us
    all_to_all x1, local copies, waits for them, and re-layouts, body(): xr = lax.all_to_all(x, 'g', 0, 1, tiled=True)  6.47 us
  transfers between devices with their start and end apart: 4, of which 1 were waited for; matrix products, arithmetic and copies ran while one was open for 8% of the time, Pallas kernels for 0%

profile of v1, /device:TPU:0, one launch (start us, length us, event | category | flops | bytes accessed | tf_op | source)
XLA Modules:
  0.0 288.7 jit_solution(4153999424893798415)
XLA Ops:
  7.2 0.0 copy-start.3
  7.2 0.0 copy-start.4
  7.2 0.0 copy-start.2
  7.2 0.0 copy-start.5
  7.2 0.0 copy-start.6
  7.2 0.0 copy-start.7
  7.2 0.0 copy-start.8
  7.2 7.5 %all-to-all-start = ((bf16[32,512,128]{2,1,0:T(8,128)(2,1)}), bf16[32,512,128]{2,1,0:T(8,128)(2,1)}, u32[]{:S(2)}, u32[]{:S(2)}) async-start(bf16[32,512,128]{2,1,0:T(8,128)(2,1)} %bitcast.39), calls=%async_computation | async-start | bytes 8388608 | tf_op jit(solution)/shard_map/all_to_all | solution.py:294
  14.7 0.0 all-gather.2.cloned.1.call-start
  14.8 0.0 copy-done.3
  14.8 0.7 pad_maximum_fusion
  15.5 0.0 all-gather.2.cloned.1.call-update
  15.6 1.3 collective-permute-start.1
  16.9 3.0 %collective-permute-start = (s32[512,11]{0,1:T(8,128)S(1)}, s32[512,11]{0,1:T(8,128)S(1)}, u32[]{:S(2)}, u32[]{:S(2)}) collective-permute-start(s32[512,11]{0,1:T(8,128)S(1)} %pad_add_fusion.3), channel_id=1, source_target_pairs={{0,1},{1,2},{2,3},{3,4},{4,5},{5,6},{6,7},{7,8},{8,9},{9,10},{10,1... | collective-permute-start | bytes 67592 | tf_op jit(solution)/shard_map/ppermute | solution.py:284
  20.0 5.2 %add_convert_fusion.1.r_1_ = bf16[512,1536]{1,0:T(8,128)(2,1)} fusion(s32[512]{0:T(512)S(1)} %bitcast.48, s32[512]{0:T(512)S(1)} %bitcast.49, s32[512]{0:T(512)S(1)} %bitcast.50, s32[512]{0:T(512)S(1)} %bitcast.51, s32[512]{0:T(512)S(1)} %bitcast.52, s32[512]{0:T(512)S(1)} %bitcast.53, s32[512]{0:T(512)S(1)} %bitcast.54, s32[512]{0:T(512)S(1)} %bitcast.55, ...), kind=kLoop, calls=%fused_computation.12 | loop fusion | flops 23592960 | bytes 1593344 | tf_op jit(solution)/shard_map/convert_element_type | solution.py:299
  25.1 0.0 copy-done.6
  25.1 0.1 copy.63
  25.3 0.0 copy-done.7
  25.3 0.1 copy.64
  25.4 0.6 pad.11.r_8_
  26.0 0.6 pad.12.r_9_
  26.7 0.9 copy.65.r_3_
  27.5 0.9 copy.66.r_5_
  28.4 0.0 collective-permute-done.1
  28.4 0.0 collective-permute-done
  28.4 0.3 copy.61
  28.7 0.3 compare_reduce_fusion
  29.0 0.2 slice_reduce_fusion.9
  29.2 1.0 maximum_convert_fusion.r_4_
  30.2 5.1 %add_convert_fusion.r_2_ = bf16[512,1536]{1,0:T(8,128)(2,1)} fusion(s32[1536]{0:T(1024)S(1)} %get-tuple-element.20, s32[1536]{0:T(1024)S(1)} %get-tuple-element.21, s32[1536]{0:T(1024)S(1)} %get-tuple-element.22, s32[1536]{0:T(1024)S(1)} %get-tuple-element.23, s32[1536]{0:T(1024)S(1)} %get-tuple-element.24, s32[1536]{0:T(1024)S(1)} %get-tuple-element.25, ...), kind=kLoop, calls=%fused_computation.1 | loop fusion | flops 23592960 | bytes 1634304 | tf_op jit(solution)/shard_map/convert_element_type | solution.py:304
  35.2 92.0 %all-to-all-done = bf16[32,512,128]{2,1,0:T(8,128)(2,1)} async-done(((bf16[32,512,128]{2,1,0:T(8,128)(2,1)}), bf16[32,512,128]{2,1,0:T(8,128)(2,1)}, u32[]{:S(2)}, u32[]{:S(2)}) %all-to-all-start) | async-done | bytes 4194336 | tf_op jit(solution)/shard_map/all_to_all | solution.py:294
  127.2 6.5 %copy.59 = bf16[512,32,128]{0,2,1:T(8,128)(2,1)} copy(bf16[512,32,128]{2,0,1:T(8,128)(2,1)} %bitcast.1) | data formatting | bytes 8388608 | tf_op jit(solution)/shard_map/all_to_all | solution.py:294
  133.7 6.9 %convolution_bitcast_fusion.1.r_0_ = f32[512,512]{1,0:T(8,128)} fusion(bf16[4096,512]{1,0:T(8,128)(2,1)} %all-gather.2.cloned.1.call-done, bf16[512,4096]{0,1:T(8,128)(2,1)} %bitcast.37), kind=kOutput, calls=%fused_computation.23 | convolution fusion | flops 2147483648 | bytes 9437184 | tf_op jit(solution)/shard_map/dot_general | solution.py:14
  140.6 55.7 %layers.1 = (bf16[512,512]{1,0:T(8,128)(2,1)}, f32[256,512]{1,0:T(8,128)}, f32[128,512]{1,0:T(8,128)}, f32[8,128]{1,0:T(8,128)}) custom-call(f32[512,512]{1,0:T(8,128)} %convolution_bitcast_fusion.1.r_0_, bf16[512,1536]{1,0:T(8,128)(2,1)} %add_convert_fusion.1.r_1_, bf16[512,1536]{1,0:T(8,128)(2,1)} %add_convert_fusion.r_2_, f32[512,1]{1,0:T(8,128)} %copy.65.r_3_, ...), custom_call_target="tpu_custom_call" | custom-call | tf_op jit(solution)/shard_map/layers/pallas_call | solution.py:309
  196.3 1.2 slice.153
  197.5 0.9 slice.152
  198.4 0.7 pad.24.clone
  199.1 1.1 maximum_maximum_fusion
  200.3 6.7 %convolution_bitcast_fusion = f32[4096,512]{0,1:T(8,128)} fusion(bf16[512,512]{1,0:T(8,128)(2,1)} %get-tuple-element.13, bf16[512,4096]{0,1:T(8,128)(2,1)S(1)} %bitcast.38), kind=kOutput, calls=%fused_computation | convolution fusion | flops 2147483648 | bytes 13107200 | tf_op jit(solution)/shard_map/dot_general | solution.py:22
  207.0 9.0 %copy.67 = f32[4096,512]{1,0:T(8,128)} copy(f32[4096,512]{0,1:T(8,128)} %convolution_bitcast_fusion) | data formatting | bytes 16777216 | tf_op jit(solution)/shard_map/dot_general | solution.py:22
  216.0 0.9 select_maximum_fusion
  216.9 60.3 %reduce.23 = (f32[128,512]{1,0:T(8,128)}, f32[4,2,2,2,40,128]{5,4,3,2,1,0:T(8,128)}) custom-call(f32[4,2,2,2,128,512]{5,4,3,2,1,0:T(8,128)} %bitcast.36, f32[4,2,2,2,40,128]{5,4,3,2,1,0:T(8,128)} %bitcast.40), custom_call_target="tpu_custom_call" | custom-call | tf_op jit(solution)/shard_map/reduce/pallas_call | solution.py:329
  277.2 1.2 slice.193
  278.5 1.2 fusion.7
  279.6 0.6 fusion.5
  280.3 0.8 fusion
  281.1 0.0 copy-done.1
  281.1 0.7 fusion.9
  (16 shorter events, 0.2 us)
Async XLA Ops:
  7.2 7.6 %copy-start.3 = (bf16[128,256]{1,0:T(8,128)(2,1)S(1)}, bf16[128,256]{1,0:T(8,128)(2,1)}, u32[]{:S(2)}) copy-start(bf16[128,256]{1,0:T(8,128)(2,1)} %param.12) | copy-start | bytes 196612
  7.2 7.6 %copy-start.4 = (bf16[128,256]{1,0:T(8,128)(2,1)S(1)}, bf16[128,256]{1,0:T(8,128)(2,1)}, u32[]{:S(2)}) copy-start(bf16[128,256]{1,0:T(8,128)(2,1)} %param.11) | copy-start | bytes 196612
  7.2 8.3 %copy-start.2 = (s32[512,10]{0,1:T(8,128)S(1)}, s32[512,10]{0,1:T(8,128)}, u32[]{:S(2)}) copy-start(s32[512,10]{0,1:T(8,128)} %param.17) | copy-start | bytes 61444
  7.2 8.3 %copy-start.5 = (s32[512,10]{0,1:T(8,128)S(1)}, s32[512,10]{0,1:T(8,128)}, u32[]{:S(2)}) copy-start(s32[512,10]{0,1:T(8,128)} %param.18) | copy-start | bytes 61444
  7.2 17.9 %copy-start.6 = (bf16[256,47]{0,1:T(8,128)(2,1)S(1)}, bf16[256,47]{0,1:T(8,128)(2,1)}, u32[]{:S(2)}) copy-start(bf16[256,47]{0,1:T(8,128)(2,1)} %param.15) | copy-start | bytes 72196
  7.2 18.0 %copy-start.7 = (bf16[256,47]{0,1:T(8,128)(2,1)S(1)}, bf16[256,47]{0,1:T(8,128)(2,1)}, u32[]{:S(2)}) copy-start(bf16[256,47]{0,1:T(8,128)(2,1)} %param.16) | copy-start | bytes 72196
  7.2 20.3 %copy-start.8 = (s32[512]{0:T(512)S(1)}, s32[512]{0:T(512)}, u32[]{:S(2)}) copy-start(s32[512]{0:T(512)} %param.19) | copy-start | bytes 6148
  7.2 120.0 %all-to-all-start = ((bf16[32,512,128]{2,1,0:T(8,128)(2,1)}), bf16[32,512,128]{2,1,0:T(8,128)(2,1)}, u32[]{:S(2)}, u32[]{:S(2)}) async-start(bf16[32,512,128]{2,1,0:T(8,128)(2,1)} %bitcast.39), calls=%async_computation | async-start | bytes 8388608 | tf_op jit(solution)/shard_map/all_to_all | solution.py:294
  14.7 119.0 %all-gather.2.cloned.1.call-start = ((), (), s32[]{:S(2)}) async-start(), calls=%async_computation.1 | async-start | bytes 4325376 | tf_op jit(solution)/shard_map/all_gather | solution.py:295
  15.6 12.8 %collective-permute-start.1 = (s32[512,11]{0,1:T(8,128)S(1)}, s32[512,11]{0,1:T(8,128)S(1)}, u32[]{:S(2)}, u32[]{:S(2)}) collective-permute-start(s32[512,11]{0,1:T(8,128)S(1)} %pad_add_fusion.3), channel_id=1, source_target_pairs={{1,0},{2,1},{3,2},{4,3},{5,4},{6,5},{7,6},{8,7},{9,8},{10,9},{11,1... | collective-permute-start | bytes 67592 | tf_op jit(solution)/shard_map/ppermute | solution.py:284
  16.9 11.5 %collective-permute-start = (s32[512,11]{0,1:T(8,128)S(1)}, s32[512,11]{0,1:T(8,128)S(1)}, u32[]{:S(2)}, u32[]{:S(2)}) collective-permute-start(s32[512,11]{0,1:T(8,128)S(1)} %pad_add_fusion.3), channel_id=1, source_target_pairs={{0,1},{1,2},{2,3},{3,4},{4,5},{5,6},{6,7},{7,8},{8,9},{9,10},{10,1... | collective-permute-start | bytes 67592 | tf_op jit(solution)/shard_map/ppermute | solution.py:284
  140.6 59.7 %copy-start = (bf16[512,32,128]{0,2,1:T(8,128)(2,1)S(1)}, bf16[512,32,128]{0,2,1:T(8,128)(2,1)}, u32[]{:S(2)}) copy-start(bf16[512,32,128]{0,2,1:T(8,128)(2,1)} %copy.59) | copy-start | bytes 12582916
  277.2 3.9 %copy-start.1 = (f32[128,512]{1,0:T(8,128)S(1)}, f32[128,512]{1,0:T(8,128)}, u32[]{:S(2)}) copy-start(f32[128,512]{1,0:T(8,128)} %get-tuple-element.18) | copy-start | bytes 786436
Sparse Core Ops, SparseCore 0:
  19.0 94.6 all-gather.1

commit v2 on v0

v2 whole, which is shorter than its diff:
```python
import jax
import jax.numpy as jnp
from jax import lax
from jax.experimental import pallas as pl
from jax.experimental.pallas import tpu as pltpu
from jax.sharding import PartitionSpec as P

BF = jnp.bfloat16
F32 = jnp.float32
I32 = jnp.int32
MESH = pl.DeviceIdType.MESH


def _dot(a, b):
    return jnp.dot(a, b, preferred_element_type=F32)


def _dot_nt(a, b):
    return lax.dot_general(a, b, (((1,), (1,)), ((), ())), preferred_element_type=F32)


def _tdot(a, b):
    return lax.dot_general(a, b, (((0,), (0,)), ((), ())), preferred_element_type=F32)


def _split3(y):
    hi = y.astype(BF)
    rest = y - hi.astype(F32)
    mid = rest.astype(BF)
    low = (rest - mid.astype(F32)).astype(BF)
    return jnp.concatenate([hi, mid, low], axis=1)


def _sum3(y):
    c = y.shape[1] // 3
    return (y[:, 2 * c:] + y[:, c:2 * c]) + y[:, :c]


def _send(src, dst, ssem, rsem, to):
    return pltpu.make_async_remote_copy(
        src_ref=src, dst_ref=dst, send_sem=ssem, recv_sem=rsem, device_id=(to,), device_id_type=MESH)


def _step(n, classes, nodes,
          xh, ws1, wn1, ws2, wn2, ws3, wn3, nbr, nmask, tgt, lab,
          o1s, o1n, o2s, o2n, o3s, o3n, oloss,
          xb, wb, pp, pr, nx, a, bt, cx, gx, w3, w3n, h1x, h2x, d3x, d2x, d1x, dbx,
          dw, rc, rl, rr, rl2, rr2, rz, d2w, d3w, sa, sb, s1, s2, s3, s4, g,
          xl, xs_s, xs_r, w_s, w_r, p_s, p_r, h_s, h_r, e_s, e_r, c_s, c_r, r_s, r_r, q_s, q_r, t_s, t_r, u_s, u_r):
    rows, slots = nbr.shape
    hid = ws2.shape[0]
    fd = ws1.shape[0]
    me = lax.axis_index('g')
    c, x, y, z = me % 2, (me // 2) % 2, (me // 4) % 2, me // 8
    zh, zl = z // 2, z % 2
    j, first = me % 16, (z // 2) * 16
    oc, ox, oy, ozl = me + 1 - 2 * c, me + 2 - 4 * x, me + 4 - 8 * y, me + 8 - 16 * zl
    partner = me + 16 - 32 * zh
    oz = [((z + 1 + i) % 4) * 8 + me % 8 for i in range(3)]
    zs = [(z + 1 + i) % 4 for i in range(3)]
    left, right = pl.ds(0, hid), pl.ds(hid, hid)
    top, bot = pl.ds(0, rows), pl.ds(rows, rows)
    lo, own, hi = pl.ds(0, rows), pl.ds(rows, rows), pl.ds(2 * rows, rows)
    has_lo, has_hi = me > 0, me < n - 1
    done = []

    def go(cp):
        cp.start()
        done.append(cp)
        return cp

    bar = pltpu.get_barrier_semaphore()

    def greet(k, _):
        pl.semaphore_signal(bar, inc=1, device_id=(lax.rem(me + k, n),), device_id_type=MESH)
        return 0

    lax.fori_loop(1, n, greet, 0)

    def xrows(t):
        return xh.at[pl.ds(pl.multiple_of(t * rows, rows), rows)]

    mycol = pl.ds(pl.multiple_of(j * fd, fd), fd)
    keep = [pltpu.make_async_copy(xrows(partner), xb.at[bot, mycol], xl.at[0]),
            pltpu.make_async_copy(xrows(me), xb.at[top, mycol], xl.at[1])]
    for cp in keep:
        cp.start()
    wb[zl, y, x, c, :, left] = ws1[...]
    wb[zl, y, x, c, :, right] = wn1[...]
    pl.semaphore_wait(bar, n - 1)

    def xcopy(s, k):
        t = first + lax.rem(j + k, 16)
        if s == 0:
            return _send(xrows(t + 16 - 32 * zh), xb.at[bot, mycol], xs_s.at[0, k], xs_r.at[0, k], t)
        return _send(xrows(t), xb.at[top, mycol], xs_s.at[1, k], xs_r.at[1, k], t)

    def xgo(s, k0, k1):
        def one(k, _):
            xcopy(s, k).start()
            return 0

        lax.fori_loop(k0, k1, one, 0)

    def xarrive(s):
        def one(k, _):
            xcopy(s, k).wait_recv()
            return 0

        lax.fori_loop(1, 16, one, 0)

    def wsend(i, src, to):
        return go(_send(src, src, w_s.at[i], w_r.at[i], to))

    f1 = wsend(0, wb.at[zl, y, x, c, :, left], ozl)
    f2 = wsend(1, wb.at[zl, y, x, c, :, right], ox)
    xgo(0, 1, 6)
    f1.wait_recv()
    f1 = wsend(2, wb.at[:, y, x, c, :, left], oy)
    f2.wait_recv()
    f2 = wsend(3, wb.at[zl, y, :, c, :, right], oy)
    xgo(0, 6, 11)
    f1.wait_recv()
    f1 = wsend(4, wb.at[:, :, x, c, :, left], ox)
    f2.wait_recv()
    f2 = wsend(5, wb.at[zl, :, :, c, :, right], ozl)
    xgo(0, 11, 16)
    xgo(1, 1, 16)

    def copies(buf, e):
        return (_send(buf.at[own], buf.at[hi], h_s.at[e, 0], h_r.at[e, 0], me - 1),
                _send(buf.at[own], buf.at[lo], h_s.at[e, 1], h_r.at[e, 1], me + 1))

    def hstart(buf, e):
        dn, up = copies(buf, e)

        @pl.when(has_lo)
        def _():
            dn.start()

        @pl.when(has_hi)
        def _():
            up.start()

    def harrive(buf, e):
        dn, up = copies(buf, e)

        @pl.when(has_hi)
        def _():
            dn.wait_recv()

        @pl.when(has_lo)
        def _():
            up.wait_recv()

    def hdrain(buf, e):
        dn, up = copies(buf, e)

        @pl.when(has_lo)
        def _():
            dn.wait_send()

        @pl.when(has_hi)
        def _():
            up.wait_send()

    def gcopies():
        return (_send(gx.at[1], gx.at[2], h_s.at[7, 0], h_r.at[7, 0], me - 1),
                _send(gx.at[1], gx.at[0], h_s.at[7, 1], h_r.at[7, 1], me + 1))

    bufs = (nx, h1x, h2x, d3x, d2x, d1x, cx)

    @pl.when(jnp.logical_not(has_lo))
    def _():
        for b in bufs:
            b[lo] = jnp.ones((rows, b.shape[1]), b.dtype)
        gx[0] = jnp.full(gx.shape[1:], -1, I32)

    @pl.when(jnp.logical_not(has_hi))
    def _():
        for b in bufs:
            b[hi] = jnp.ones((rows, b.shape[1]), b.dtype)
        gx[2] = jnp.full(gx.shape[1:], -1, I32)

    base = me * rows
    cnt = jnp.sum(nmask[...].astype(F32), axis=1, keepdims=True)
    cx[own] = jnp.broadcast_to(cnt, (rows, 128)).astype(BF)
    hstart(cx, 6)
    tg = tgt[...]
    tin = (tg >= base) & (tg < base + rows)
    tout = jnp.where((tg >= 0) & jnp.logical_not(tin), tg + 1, 0)
    trem = tout[0:1]
    for k in range(1, slots):
        trem = trem + tout[k:k + 1]
    gx[1] = jnp.broadcast_to(trem - 1, gx.shape[1:])
    gdn, gup = gcopies()

    @pl.when(has_lo)
    def _():
        gdn.start()

    @pl.when(has_hi)
    def _():
        gup.start()

    f1.wait_recv()
    f2.wait_recv()
    fw = wsend(6, wb.at[:, :, :, c], oc)

    loc = nbr[...] - base
    ok = nmask[...] > 0
    inside = (loc >= 0) & (loc < rows)
    lin = jnp.where(ok & inside, loc, -1)
    rem = (jnp.sum(jnp.where(ok & jnp.logical_not(inside), loc + rows + 1, 0).astype(F32), axis=1, keepdims=True)
           - 1.0).astype(I32)
    col = lax.broadcasted_iota(I32, (rows, rows), 1)
    a[:, lo] = (rem == col).astype(F32).astype(BF)
    a[:, hi] = (rem == col + 2 * rows).astype(F32).astype(BF)
    acc = jnp.zeros((rows, rows), F32)
    for k in range(slots):
        acc = acc + (lin[:, k:k + 1] == col).astype(F32)
    a[:, own] = acc.astype(BF)
    row = lax.broadcasted_iota(I32, (rows, rows), 0)
    tloc = jnp.where(tin, tg - base, -1)
    acc = jnp.zeros((rows, rows), F32)
    for k in range(slots):
        acc = acc + (tloc[k:k + 1] == row).astype(F32)
    bt[:, own] = acc.astype(BF)
    gdn, gup = gcopies()

    @pl.when(has_hi)
    def _():
        gdn.wait_recv()

    @pl.when(has_lo)
    def _():
        gup.wait_recv()

    bt[:, lo] = ((gx[0, 0:1] - base) == row).astype(F32).astype(BF)
    bt[:, hi] = ((gx[2, 0:1] - base) == row).astype(F32).astype(BF)
    w3[...] = jnp.zeros(w3.shape, BF)
    w3n[...] = jnp.zeros(w3n.shape, BF)
    w3[:, :classes] = ws3[...]
    w3n[:, :classes] = wn3[...]
    harrive(cx, 6)
    cntx = cx[:, 0:1].astype(F32)

    fw.wait_recv()
    keep[0].wait()
    xarrive(0)
    wall = wb[...].reshape(16 * fd, 2 * hid)
    pp[:, right] = _dot(xb[bot], wall[:, hid:])
    cn = go(_send(pp.at[:, right], pr.at[:, right], p_s.at[0], p_r.at[0], partner))
    pp[:, left] = _dot(xb[bot], wall[:, :hid])
    cs = go(_send(pp.at[:, left], pr.at[:, left], p_s.at[1], p_r.at[1], partner))
    keep[1].wait()
    xarrive(1)
    po = _dot(xb[top], wb[...].reshape(16 * fd, 2 * hid))
    cn.wait_recv()
    nx[own] = po[:, hid:] + pr[:, right]
    hstart(nx, 0)
    acc = _sum3(_dot(a[:, own], _split3(nx[own])))
    harrive(nx, 0)
    acc = acc + _sum3(_dot(a[:, lo], _split3(nx[lo]))) + _sum3(_dot(a[:, hi], _split3(nx[hi])))
    acc = po[:, :hid] + acc / cnt
    cs.wait_recv()
    z1 = acc + pr[:, left]
    h1 = jnp.maximum(z1, 0.0).astype(BF)
    h1x[own] = h1
    hstart(h1x, 1)

    z2 = _dot(h1, ws2[...])
    harrive(h1x, 1)
    m1 = (_dot(a[...], h1x[...]) / cnt).astype(BF)
    z2 = z2 + _dot(m1, wn2[...])
    h2 = jnp.maximum(z2, 0.0).astype(BF)
    h2x[own] = h2
    hstart(h2x, 2)
    logits = _dot(h2, w3[...])
    harrive(h2x, 2)
    m2 = (_dot(a[...], h2x[...]) / cnt).astype(BF)
    logits = logits + _dot(m2, w3n[...])
    cls = lax.broadcasted_iota(I32, logits.shape, 1)
    real = cls < classes
    peak = jnp.max(jnp.where(real, logits, -jnp.inf), axis=1, keepdims=True)
    ex = jnp.where(real, jnp.exp(logits - peak), 0.0)
    tot = jnp.sum(ex, axis=1, keepdims=True)
    hot = cls == lab[...]
    picked = jnp.sum(jnp.where(hot, logits, 0.0), axis=1, keepdims=True)
    loss = jnp.sum(jnp.log(tot) + peak - picked, axis=0, keepdims=True) / nodes
    d3 = ((ex / tot - hot.astype(F32)) / nodes).astype(BF)
    d3x[own] = d3
    hstart(d3x, 3)
    d3w[:, left] = _tdot(d3, h2)
    d3w[:, right] = _tdot(d3, m2)
    d3w[48:56] = jnp.broadcast_to(loss, (8, 2 * hid))
    d2 = _dot_nt(d3, w3[...])
    harrive(d3x, 3)
    d2 = d2 + _sum3(_dot(bt[...], _split3(_dot_nt(d3x[...], w3n[...]) / cntx)))
    d2 = jnp.where(z2 > 0, d2, 0.0).astype(BF)
    d2x[own] = d2
    hstart(d2x, 4)
    d2w[:, left] = _tdot(h1, d2)
    d2w[:, right] = _tdot(m1, d2)

    r2, r3 = hid // 8, 8

    def place(t):
        return t // 8, (t % 8), pl.ds((t // 8) * 128, 128)

    for t in range(n):
        _, r, cb = place(t)
        at = (t // 8, (t // 4) % 2, (t // 2) % 2, t % 2)
        sa[at + (pl.ds(0, r2),)] = d2w[pl.ds(r * r2, r2), cb]
        sa[at + (pl.ds(r2, r3),)] = d3w[pl.ds(r * r3, r3), cb]

    def small(i, src, dst, to):
        return go(_send(src, dst, q_s.at[i], q_r.at[i], to))

    k1 = small(0, sa.at[:, :, :, 1 - c], s1, oc)
    d1 = _dot_nt(d2, ws2[...])
    harrive(d2x, 4)
    d1 = d1 + _sum3(_dot(bt[...], _split3(_dot_nt(d2x[...], wn2[...]) / cntx)))
    d1 = jnp.where(z1 > 0, d1, 0.0).astype(BF)
    d1x[own] = d1
    hstart(d1x, 5)
    dbx[top, left] = d1
    e1 = go(_send(dbx.at[top, left], dbx.at[bot, left], e_s.at[0], e_r.at[0], partner))
    k1.wait_recv()
    sb[...] = sa[:, :, :, c] + s1[...]
    k2 = small(1, sb.at[:, :, 1 - x], s2, ox)
    harrive(d1x, 5)
    dbx[top, right] = _sum3(_dot(bt[...], _split3(d1x[...].astype(F32) / cntx))).astype(BF)
    e2 = go(_send(dbx.at[top, right], dbx.at[bot, right], e_s.at[1], e_r.at[1], partner))
    k2.wait_recv()
    sb[:, :, x] = sb[:, :, x] + s2[...]
    k3 = small(2, sb.at[:, 1 - y, x], s3, oy)

    qs = [1 - zl, zl]
    wide = 8 * fd

    def feats(q):
        return pl.ds(pl.multiple_of(q * wide, wide), wide)

    def grid(v):
        return v.reshape(2, 2, 2, fd, 2 * hid)

    for q in qs:
        dw[q] = grid(_tdot(xb[top, feats(q)], dbx[top]))
    k3.wait_recv()
    sb[:, y, x] = sb[:, y, x] + s3[...]
    k4 = [go(_send(sb.at[zs[i], y, x], s4.at[i], t_s.at[i], t_r.at[i], oz[i])) for i in range(3)]
    e1.wait_recv()
    e2.wait_recv()
    cores = []
    for i, q in enumerate(qs):
        dw[q] = dw[q] + grid(_tdot(xb[bot, feats(q)], dbx[bot]))
        cores.append(go(_send(dw.at[q, :, :, 1 - c], rc.at[q], c_s.at[i], c_r.at[i], oc)))
    one, two = [], []

    def step1(i):
        q = qs[i]
        cores[i].wait_recv()
        dw[q, :, :, c] = dw[q, :, :, c] + rc[q]
        one.append((
            go(_send(dw.at[q, :, 1 - x, c, :, left], rl.at[q], r_s.at[0, i], r_r.at[0, i], ox)),
            go(_send(dw.at[q, 1 - y, :, c, :, right], rr.at[q], r_s.at[1, i], r_r.at[1, i], oy))))

    def step2(i):
        q = qs[i]
        for cp in one[i]:
            cp.wait_recv()
        dw[q, :, x, c, :, left] = dw[q, :, x, c, :, left] + rl[q]
        dw[q, y, :, c, :, right] = dw[q, y, :, c, :, right] + rr[q]
        two.append((
            go(_send(dw.at[q, 1 - y, x, c, :, left], rl2.at[q], r_s.at[2, i], r_r.at[2, i], oy)),
            go(_send(dw.at[q, y, 1 - x, c, :, right], rr2.at[q], r_s.at[3, i], r_r.at[3, i], ox))))

    def step3(i):
        q = qs[i]
        for cp in two[i]:
            cp.wait_recv()
        dw[q, y, x, c, :, left] = dw[q, y, x, c, :, left] + rl2[q]
        dw[q, y, x, c, :, right] = dw[q, y, x, c, :, right] + rr2[q]

    step1(0)
    step1(1)
    for cp in k4:
        cp.wait_recv()
    g[z, y, x, c] = ((sb[z, y, x] + s4[0]) + s4[1]) + s4[2]
    k5 = [go(_send(g.at[z, y, x, c], g.at[z, y, x, c], u_s.at[i], u_r.at[i], oz[i])) for i in range(3)]
    step2(0)
    for cp in k5:
        cp.wait_recv()
    k6 = small(3, g.at[:, y, x, c], g.at[:, y, x, c], oy)
    step2(1)
    step3(0)
    last = go(_send(dw.at[qs[0], y, x, c], rz, c_s.at[2], c_r.at[2], ozl))
    k6.wait_recv()
    k7 = small(4, g.at[:, :, x, c], g.at[:, :, x, c], ox)
    step3(1)
    k7.wait_recv()
    k8 = small(5, g.at[:, :, :, c], g.at[:, :, :, c], oc)
    k8.wait_recv()
    for t in range(n):
        cbi, r, _ = place(t)
        v = g[t // 8, (t // 4) % 2, (t // 2) % 2, t % 2]
        o = o2s if cbi < 2 else o2n
        o[pl.ds(r * r2, r2), pl.ds((cbi % 2) * 128, 128)] = v[:r2]
        d3w[pl.ds(r * r3, r3), pl.ds(cbi * 128, 128)] = v[r2:]
    oloss[...] = d3w[48:56, :128]
    o3s[...] = d3w[:, left].T[:, :classes]
    o3n[...] = d3w[:, right].T[:, :classes]
    last.wait_recv()
    o1s[...] = dw[zl, y, x, c, :, left] + rz[:, left]
    o1n[...] = dw[zl, y, x, c, :, right] + rz[:, right]

    for e, b in enumerate(bufs):
        hdrain(b, e)
    gdn, gup = gcopies()

    @pl.when(has_lo)
    def _():
        gdn.wait_send()

    @pl.when(has_hi)
    def _():
        gup.wait_send()

    for s in range(2):
        def drain(k, _):
            xcopy(s, k).wait_send()
            return 0

        lax.fori_loop(1, 16, drain, 0)
    for cp in done:
        cp.wait_send()


def solution(mesh):
    n = mesh.shape['g']
    vm = pl.BlockSpec(memory_space=pltpu.VMEM)
    hbm = pl.BlockSpec(memory_space=pl.ANY)
    dma = pltpu.SemaphoreType.DMA
    sds = jax.ShapeDtypeStruct

    def body(x, ws1, wn1, ws2, wn2, ws3, wn3, nbr, nmask, labels):
        nodes = x.shape[0]
        rows = nbr.shape[0]
        fd, hid = ws1.shape
        classes = ws3.shape[1]
        per = hid // 8 + 8
        w = 2 * hid
        v = pltpu.VMEM
        tgt = jnp.where(nmask > 0, nbr, -1).T
        scratch = [
            v((2 * rows, 16 * fd), BF), v((2, 2, 2, 2, fd, w), BF), v((rows, w), F32), v((rows, w), F32),
            v((3 * rows, hid), F32), v((rows, 3 * rows), BF), v((rows, 3 * rows), BF), v((3 * rows, 128), BF),
            v((3, 8, rows), I32), v((hid, 128), BF), v((hid, 128), BF),
            v((3 * rows, hid), BF), v((3 * rows, hid), BF), v((3 * rows, 128), BF), v((3 * rows, hid), BF),
            v((3 * rows, hid), BF), v((2 * rows, w), BF),
            v((2, 2, 2, 2, fd, w), F32), v((2, 2, 2, fd, w), F32), v((2, 2, fd, hid), F32), v((2, 2, fd, hid), F32),
            v((2, fd, hid), F32), v((2, fd, hid), F32), v((fd, w), F32), v((hid, w), F32), v((128, w), F32),
            v((4, 2, 2, 2, per, 128), F32), v((4, 2, 2, per, 128), F32), v((4, 2, 2, per, 128), F32),
            v((4, 2, per, 128), F32), v((4, per, 128), F32), v((3, per, 128), F32), v((4, 2, 2, 2, per, 128), F32),
            dma((2,)), dma((2, 16)), dma((2, 16)), dma((7,)), dma((7,)), dma((2,)), dma((2,)), dma((8, 2)), dma((8, 2)),
            dma((2,)), dma((2,)), dma((3,)), dma((3,)), dma((4, 2)), dma((4, 2)), dma((6,)), dma((6,)),
            dma((3,)), dma((3,)), dma((3,)), dma((3,))]
        o1s, o1n, o2s, o2n, o3s, o3n, loss = pl.pallas_call(
            lambda *r: _step(n, classes, nodes, *r),
            out_shape=(sds((fd, hid), F32), sds((fd, hid), F32), sds((hid, hid), F32), sds((hid, hid), F32),
                       sds((hid, classes), F32), sds((hid, classes), F32), sds((8, 128), F32)),
            in_specs=[hbm] + [vm] * 10, out_specs=(vm,) * 7, scratch_shapes=scratch,
            compiler_params=pltpu.CompilerParams(collective_id=0, has_side_effects=True, vmem_limit_bytes=60 << 20),
            name='step',
        )(x, ws1, wn1, ws2, wn2, ws3, wn3, nbr, nmask, tgt, labels[:, None])
        return loss[0, 0], o1s, o1n, o2s, o2n, o3s, o3n

    r = P('g', None)
    in_specs = (P(None, 'g'), r, r, P(), P(), P(), P(), r, r, P('g'))
    out_specs = (P(), r, r, P(), P(), P(), P())
    return jax.shard_map(body, mesh=mesh, in_specs=in_specs, out_specs=out_specs, check_vma=False)
```

time: 3200 us -> 221 us (0.07)
  other arithmetic: 1410 us -> 1.4 us
  local copies, waits for them, and re-layouts: 810 us -> 18.6 us
  waiting for transfers between devices: 726 us -> 0 us
  Pallas kernels: 0 us -> 198 us
  blocking collectives: 130 us -> 0 us
  matrix products: 92.3 us -> 0 us
    scatter-add x30 -> x0, other arithmetic: 1390 us -> none  [_mean_nbr_t(): acc = acc.at[nbr[:, k]].add(jnp.where(nmask[:, k:k + 1] > 0, gs, 0.0))]
    gather x31 -> x0, local copies, waits for them, and re-layouts: 803 us -> none  [the longest x30 799 us: _mean_nbr(): y[nbr[:, k]].astype(jnp.float32)]
    reduce_scatter x3 -> x0, waiting for transfers between devices: 547 us -> none  [the longest x1 185 us: body(): lax.psum_scatter(_mean_nbr_t(_dot(d2, wn2.T), nbr, nmask, nodes), 'g', sc...]
    pallas_call x0 -> x1, Pallas kernels: none -> 198 us  [body(): pl.pallas_call(lambda *r: _step(n, classes, nodes, *r), out_shape=(sds((f...]
    all_gather x3 -> x0, waiting for transfers between devices: 179 us -> none  [the longest x1 77.9 us: body(): lax.all_gather(h1, 'g', axis=0, tiled=True)]
    dot_general x16 -> x0, matrix products: 92.3 us -> none  [the longest x10 74.8 us: _dot(): return jnp.dot(a, b, preferred_element_type=jnp.float32)]
    all_gather x2 -> x0, blocking collectives: 85.6 us -> none  [the longest x1 46.1 us: body(): nbr_all = lax.all_gather(nbr, 'g', axis=0, tiled=True)]
    psum x1 -> x0, blocking collectives: 44.4 us -> none  [body(): loss = lax.psum(jnp.sum(lse - picked), 'g') / nodes]
  transfers between devices with their start and end apart: 7 -> 0, of which waited for: 6 -> 0; matrix products, arithmetic and copies ran while one was open for 36% -> 0% of each run, Pallas kernels for 0% -> 0%
where the time goes in v2:
time: 221 us; the launch traced here: 219 us
  Pallas kernels  198 us (90%)
  local copies, waits for them, and re-layouts  18.6 us (8%)
    pallas_call x1, Pallas kernels, body(): pl.pallas_call(lambda *r: _step(n, classes, nodes, *r), out_shape=(sds((f...  198 us
    unnamed x10, local copies, waits for them, and re-layouts  15.9 us

profile of v2, /device:TPU:0, one launch (start us, length us, event | category | flops | bytes accessed | tf_op | source)
XLA Modules:
  0.0 219.1 jit_solution(7388737189674745780)
XLA Ops:
  0.6 1.4 select_bitcast_fusion.r_9_
  2.0 1.5 copy.23.r_5_
  3.5 1.5 copy.24.r_6_
  5.0 1.5 copy.27.r_10_
  6.5 1.6 copy.25.r_7_
  8.1 1.6 copy.26.r_8_
  9.7 198.5 %step.1 = (f32[128,256]{1,0:T(8,128)}, f32[128,256]{1,0:T(8,128)}, f32[256,256]{1,0:T(8,128)}, f32[256,256]{1,0:T(8,128)}, f32[256,47]{1,0:T(8,128)}, /*index=5*/f32[256,47]{1,0:T(8,128)}, f32[8,128]{1,0:T(8,128)}) custom-call(bf16[16384,128]{1,0:T(8,128)(2,1)} %r_0_.1, bf16[128,256]{1,0:T(8,128)(2,1)} %r_1_.1, bf16[128,256]{1,0:T(8,128)(2,1)} %r_2_.1, ...), custom_call_target="tpu_custom_call" | custom-call | tf_op jit(solution)/shard_map/step/pallas_call | solution.py:469
  208.2 1.2 slice.3
  209.4 1.6 copy.28
  211.0 1.6 copy.29
  212.6 1.6 copy.34
  214.2 1.6 copy.35
  215.7 1.7 copy.36
  217.4 1.7 copy.37

commit v3 on v2

v3 whole, which is shorter than its diff:
```python
import jax
import jax.numpy as jnp
from jax import lax
from jax.experimental import pallas as pl
from jax.experimental.pallas import tpu as pltpu
from jax.sharding import PartitionSpec as P

BF = jnp.bfloat16
F32 = jnp.float32
I32 = jnp.int32
MESH = pl.DeviceIdType.MESH


def _dot(a, b):
    return jnp.dot(a, b, preferred_element_type=F32)


def _dot_nt(a, b):
    return lax.dot_general(a, b, (((1,), (1,)), ((), ())), preferred_element_type=F32)


def _tdot(a, b):
    return lax.dot_general(a, b, (((0,), (0,)), ((), ())), preferred_element_type=F32)


def _split3(y):
    hi = y.astype(BF)
    rest = y - hi.astype(F32)
    mid = rest.astype(BF)
    low = (rest - mid.astype(F32)).astype(BF)
    return jnp.concatenate([hi, mid, low], axis=1)


def _sum3(y):
    c = y.shape[1] // 3
    return (y[:, 2 * c:] + y[:, c:2 * c]) + y[:, :c]


def _send(src, dst, ssem, rsem, to):
    return pltpu.make_async_remote_copy(
        src_ref=src, dst_ref=dst, send_sem=ssem, recv_sem=rsem, device_id=(to,), device_id_type=MESH)


def _step(n, classes, nodes,
          xh, ws1, wn1, ws2, wn2, ws3, wn3, nbr, nmask, lab,
          o1s, o1n, o2s, o2n, o3s, o3n, oloss,
          xb, wb, pp, pr, nx, a, bt, cx, gx, w3, w3n, h1x, h2x, d3x, d2x, d1x, dbx,
          dw, rc, r1, r2, rz, d2w, d3w, gt, sa, sb, s1, s2, s3, s4, g,
          xl, xs_s, xs_r, w_s, w_r, p_s, p_r, h_s, h_r, e_s, e_r, c_s, c_r, r_s, r_r, q_s, q_r, t_s, t_r, u_s, u_r):
    slots, rows = nbr.shape
    hid = ws2.shape[0]
    fd = ws1.shape[0]
    me = lax.axis_index('g')
    c, x, y, z = me % 2, (me // 2) % 2, (me // 4) % 2, me // 8
    zh, zl = z // 2, z % 2
    j, first = me % 16, (z // 2) * 16
    oc, ox, oy, ozl = me + 1 - 2 * c, me + 2 - 4 * x, me + 4 - 8 * y, me + 8 - 16 * zl
    partner = me + 16 - 32 * zh
    oz = [((z + 1 + i) % 4) * 8 + me % 8 for i in range(3)]
    zs = [(z + 1 + i) % 4 for i in range(3)]
    left, right = pl.ds(0, hid), pl.ds(hid, hid)
    top, bot = pl.ds(0, rows), pl.ds(rows, rows)
    lo, own, hi = pl.ds(0, rows), pl.ds(rows, rows), pl.ds(2 * rows, rows)
    has_lo, has_hi = me > 0, me < n - 1
    done = []

    def go(cp):
        cp.start()
        done.append(cp)
        return cp

    bar = pltpu.get_barrier_semaphore()

    def greet(k, _):
        pl.semaphore_signal(bar, inc=1, device_id=(lax.rem(me + k, n),), device_id_type=MESH)
        return 0

    lax.fori_loop(1, n, greet, 0)

    def xrows(t):
        return xh.at[pl.ds(pl.multiple_of(t * rows, rows), rows)]

    mycol = pl.ds(pl.multiple_of(j * fd, fd), fd)
    keep = [pltpu.make_async_copy(xrows(partner), xb.at[bot, mycol], xl.at[0]),
            pltpu.make_async_copy(xrows(me), xb.at[top, mycol], xl.at[1])]
    for cp in keep:
        cp.start()
    wb[zl, y, x, c, :, left] = ws1[...]
    wb[zl, y, x, c, :, right] = wn1[...]
    pl.semaphore_wait(bar, n - 1)

    part = rows // 2

    def xcopy(s, k):
        t = first + jnp.bitwise_xor(j, k)
        if s < 2:
            r = (t + 16 - 32 * zh) * rows + s * part
            to = pl.ds(rows + s * part, part)
            size = part
        else:
            r, to, size = t * rows, top, rows
        return _send(xh.at[pl.ds(pl.multiple_of(r, part), size)], xb.at[to, mycol], xs_s.at[s, k], xs_r.at[s, k], t)

    order = (1, 2, 4, 8, 3, 5, 9, 14, 15, 6, 10, 12, 7, 11, 13)

    def xgo(s, ks):
        for k in ks:
            xcopy(s, k).start()

    def xarrive(s):
        def one(k, _):
            xcopy(s, k).wait_recv()
            return 0

        lax.fori_loop(1, 16, one, 0)

    def wsend(i, src, to):
        return go(_send(src, src, w_s.at[i], w_r.at[i], to))

    oxy = first + jnp.bitwise_xor(j, 6)
    oxz = first + jnp.bitwise_xor(j, 10)
    mine_l, mine_r = wb.at[zl, y, x, c, :, left], wb.at[zl, y, x, c, :, right]
    fl = [wsend(0, mine_l, ox), wsend(1, mine_l, oy), wsend(2, mine_l, oxy)]
    fr = [wsend(4, mine_r, ozl), wsend(3, mine_r, ox), wsend(5, mine_r, oxz)]
    xgo(0, order[:7])

    def copies(buf, e):
        return (_send(buf.at[own], buf.at[hi], h_s.at[e, 0], h_r.at[e, 0], me - 1),
                _send(buf.at[own], buf.at[lo], h_s.at[e, 1], h_r.at[e, 1], me + 1))

    def hstart(buf, e):
        dn, up = copies(buf, e)

        @pl.when(has_lo)
        def _():
            dn.start()

        @pl.when(has_hi)
        def _():
            up.start()

    def harrive(buf, e):
        dn, up = copies(buf, e)

        @pl.when(has_hi)
        def _():
            dn.wait_recv()

        @pl.when(has_lo)
        def _():
            up.wait_recv()

    def hdrain(buf, e):
        dn, up = copies(buf, e)

        @pl.when(has_lo)
        def _():
            dn.wait_send()

        @pl.when(has_hi)
        def _():
            up.wait_send()

    def gcopies():
        return (_send(gx.at[1], gx.at[2], h_s.at[7, 0], h_r.at[7, 0], me - 1),
                _send(gx.at[1], gx.at[0], h_s.at[7, 1], h_r.at[7, 1], me + 1))

    bufs = (nx, h1x, h2x, d3x, d2x, d1x, cx)

    @pl.when(jnp.logical_not(has_lo))
    def _():
        for b in bufs:
            b[lo] = jnp.ones((rows, b.shape[1]), b.dtype)
        gx[0] = jnp.full(gx.shape[1:], -1, I32)

    @pl.when(jnp.logical_not(has_hi))
    def _():
        for b in bufs:
            b[hi] = jnp.ones((rows, b.shape[1]), b.dtype)
        gx[2] = jnp.full(gx.shape[1:], -1, I32)

    base = me * rows
    nb, ok = nbr[...], nmask[...] > 0
    tin = ok & (nb >= base) & (nb < base + rows)
    tloc = jnp.where(tin, nb - base, -1)
    tout = jnp.where(ok & jnp.logical_not(tin), nb + 1, 0)
    tcnt = nmask[...]
    trem, tc = tout[0:1], tcnt[0:1]
    for k in range(1, slots):
        trem = trem + tout[k:k + 1]
        tc = tc + tcnt[k:k + 1]
    gx[1] = jnp.broadcast_to(trem - 1, gx.shape[1:])
    gt[...] = jnp.zeros(gt.shape, F32)
    gt[0:slots] = tloc.astype(F32)
    gt[slots:slots + 1] = jnp.where(trem > 0, trem - 1 - base + rows, -1).astype(F32)
    gt[slots + 1:slots + 2] = tc.astype(F32)
    gt[slots + 2:slots + 3] = lab[...].astype(F32)
    gc = gt[...].T
    cnt = gc[:, slots + 1:slots + 2]
    labc = gc[:, slots + 2:slots + 3].astype(I32)
    cx[own] = jnp.broadcast_to(cnt, (rows, 128)).astype(BF)
    hstart(cx, 6)
    gdn, gup = gcopies()

    @pl.when(has_lo)
    def _():
        gdn.start()

    @pl.when(has_hi)
    def _():
        gup.start()

    for f in fl:
        f.wait_recv()
    fl = wsend(6, wb.at[zl, :, :, c, :, left], ozl)
    for f in fr:
        f.wait_recv()
    fr = wsend(7, wb.at[:, y, :, c, :, right], oy)
    xgo(0, order[7:])
    lin = gc[:, 0:slots].astype(I32)
    rem = gc[:, slots:slots + 1].astype(I32)
    col = lax.broadcasted_iota(I32, (rows, rows), 1)
    acc = jnp.zeros((rows, rows), F32)
    for k in range(slots):
        acc = acc + (lin[:, k:k + 1] == col).astype(F32)
    a[:, own] = acc.astype(BF)
    xgo(1, order)
    row = lax.broadcasted_iota(I32, (rows, rows), 0)
    acc = jnp.zeros((rows, rows), F32)
    for k in range(slots):
        acc = acc + (tloc[k:k + 1] == row).astype(F32)
    bt[:, own] = acc.astype(BF)
    fr.wait_recv()
    fr = wsend(8, wb.at[:, :, :, c, :, right], oc)
    fl.wait_recv()
    fl = wsend(9, wb.at[:, :, :, c, :, left], oc)
    keep[0].wait()
    xarrive(0)
    xgo(2, order)

    fr.wait_recv()
    fl.wait_recv()
    p1, p2 = pl.ds(0, part), pl.ds(part, part)
    f1, f2 = pl.ds(rows, part), pl.ds(rows + part, part)

    def wcols(cols):
        return wb[:, :, :, :, :, cols].reshape(16 * fd, hid)

    def swap(i, rs, cols):
        return go(_send(pp.at[rs, cols], pr.at[rs, cols], p_s.at[i], p_r.at[i], partner))

    pp[p1, right] = _dot(xb[f1], wcols(right))
    cn1 = swap(0, p1, right)
    pp[p1, left] = _dot(xb[f1], wcols(left))
    cs1 = swap(2, p1, left)
    a[:, lo] = (rem == col).astype(F32).astype(BF)
    a[:, hi] = (rem == col + 2 * rows).astype(F32).astype(BF)
    gdn, gup = gcopies()

    @pl.when(has_hi)
    def _():
        gdn.wait_recv()

    @pl.when(has_lo)
    def _():
        gup.wait_recv()

    bt[:, lo] = ((gx[0, 0:1] - base) == row).astype(F32).astype(BF)
    bt[:, hi] = ((gx[2, 0:1] - base) == row).astype(F32).astype(BF)
    w3[...] = jnp.zeros(w3.shape, BF)
    w3n[...] = jnp.zeros(w3n.shape, BF)
    w3[:classes] = ws3[...]
    w3n[:classes] = wn3[...]
    harrive(cx, 6)

    def back(at, v):
        return _sum3(_dot(bt[:, at], _split3(v / cx[at, 0:1].astype(F32))))

    xarrive(1)
    pp[p2, right] = _dot(xb[f2], wcols(right))
    cn2 = swap(1, p2, right)
    pp[p2, left] = _dot(xb[f2], wcols(left))
    cs2 = swap(3, p2, left)
    keep[1].wait()
    xarrive(2)
    po = _dot(xb[top], wcols(right))
    cn1.wait_recv()
    cn2.wait_recv()
    nx[own] = po + pr[:, right]
    hstart(nx, 0)
    po = _dot(xb[top], wcols(left))
    acc = _sum3(_dot(a[:, own], _split3(nx[own])))
    harrive(nx, 0)
    acc = acc + _sum3(_dot(a[:, lo], _split3(nx[lo]))) + _sum3(_dot(a[:, hi], _split3(nx[hi])))
    acc = po + acc / cnt
    cs1.wait_recv()
    cs2.wait_recv()
    z1 = acc + pr[:, left]
    h1 = jnp.maximum(z1, 0.0).astype(BF)
    h1x[own] = h1
    hstart(h1x, 1)

    z2 = _dot(h1, ws2[...])
    m1 = _dot(a[:, own], h1)
    harrive(h1x, 1)
    m1 = ((m1 + _dot(a[:, lo], h1x[lo]) + _dot(a[:, hi], h1x[hi])) / cnt).astype(BF)
    z2 = z2 + _dot(m1, wn2[...])
    h2 = jnp.maximum(z2, 0.0).astype(BF)
    h2x[own] = h2
    hstart(h2x, 2)
    logits = _dot_nt(h2, w3[...])
    m2 = _dot(a[:, own], h2)
    harrive(h2x, 2)
    m2 = ((m2 + _dot(a[:, lo], h2x[lo]) + _dot(a[:, hi], h2x[hi])) / cnt).astype(BF)
    logits = logits + _dot_nt(m2, w3n[...])
    cls = lax.broadcasted_iota(I32, logits.shape, 1)
    real = cls < classes
    peak = jnp.max(jnp.where(real, logits, -jnp.inf), axis=1, keepdims=True)
    ex = jnp.where(real, jnp.exp(logits - peak), 0.0)
    tot = jnp.sum(ex, axis=1, keepdims=True)
    hot = cls == labc
    picked = jnp.sum(jnp.where(hot, logits, 0.0), axis=1, keepdims=True)
    loss = jnp.sum(jnp.log(tot) + peak - picked, axis=0, keepdims=True) / nodes
    d3 = ((ex / tot - hot.astype(F32)) / nodes).astype(BF)
    d3x[own] = d3
    hstart(d3x, 3)
    d3w[:, left] = _tdot(d3, h2)
    d3w[:, right] = _tdot(d3, m2)
    d3w[48:56] = jnp.broadcast_to(loss, (8, 2 * hid))
    d2 = _dot(d3, w3[...])
    d2 = d2 + back(own, _dot(d3, w3n[...]))
    harrive(d3x, 3)
    d2 = d2 + back(lo, _dot(d3x[lo], w3n[...])) + back(hi, _dot(d3x[hi], w3n[...]))
    d2 = jnp.where(z2 > 0, d2, 0.0).astype(BF)
    d2x[own] = d2
    hstart(d2x, 4)
    d2w[:, left] = _tdot(h1, d2)
    d2w[:, right] = _tdot(m1, d2)

    h2r, h3r = hid // 8, 8

    def place(t):
        return t // 8, (t % 8), pl.ds((t // 8) * 128, 128)

    for t in range(n):
        _, r, cb = place(t)
        at = (t // 8, (t // 4) % 2, (t // 2) % 2, t % 2)
        sa[at + (pl.ds(0, h2r),)] = d2w[pl.ds(r * h2r, h2r), cb]
        sa[at + (pl.ds(h2r, h3r),)] = d3w[pl.ds(r * h3r, h3r), cb]

    def small(i, src, dst, to):
        return go(_send(src, dst, q_s.at[i], q_r.at[i], to))

    k1 = small(0, sa.at[:, :, :, 1 - c], s1, oc)
    d1 = _dot_nt(d2, ws2[...])
    d1 = d1 + back(own, _dot_nt(d2, wn2[...]))
    harrive(d2x, 4)
    d1 = d1 + back(lo, _dot_nt(d2x[lo], wn2[...])) + back(hi, _dot_nt(d2x[hi], wn2[...]))
    d1 = jnp.where(z1 > 0, d1, 0.0).astype(BF)
    d1x[own] = d1
    hstart(d1x, 5)
    dbx[top, left] = d1
    e1 = go(_send(dbx.at[top, left], dbx.at[bot, left], e_s.at[0], e_r.at[0], partner))
    b1 = back(own, d1.astype(F32))
    k1.wait_recv()
    sb[...] = sa[:, :, :, c] + s1[...]
    k2 = small(1, sb.at[:, :, 1 - x], s2, ox)
    harrive(d1x, 5)
    b1 = b1 + back(lo, d1x[lo].astype(F32)) + back(hi, d1x[hi].astype(F32))
    dbx[top, right] = b1.astype(BF)
    e2 = go(_send(dbx.at[top, right], dbx.at[bot, right], e_s.at[1], e_r.at[1], partner))
    k2.wait_recv()
    sb[:, :, x] = sb[:, :, x] + s2[...]
    k3 = small(2, sb.at[:, 1 - y, x], s3, oy)

    qs = [1 - zl, zl]
    wide = 8 * fd

    def feats(q):
        return pl.ds(pl.multiple_of(q * wide, wide), wide)

    units = [(i, m) for m in range(2) for i in range(2)]
    side = [left, right]

    def own_grad(u):
        i, m = units[u]
        q = qs[i]
        v = _tdot(xb[:, feats(q)], dbx[:, side[m]])
        dw[q, :, :, :, :, side[m]] = v.reshape(2, 2, 2, fd, hid)
        return go(_send(dw.at[q, :, :, 1 - c, :, side[m]], rc.at[q, :, :, :, side[m]], c_s.at[u], c_r.at[u], oc))

    one, two, three = {}, {}, {}

    def step1(u):
        i, m = units[u]
        q, sm = qs[i], side[m]
        cores[u].wait_recv()
        dw[q, :, :, c, :, sm] = dw[q, :, :, c, :, sm] + rc[q, :, :, :, sm]
        if i == 0:
            one[u] = go(_send(dw.at[q, :, 1 - x, c, :, sm], r1.at[u], r_s.at[0, u], r_r.at[0, u], ox))
        else:
            one[u] = go(_send(dw.at[q, 1 - y, :, c, :, sm], r1.at[u], r_s.at[0, u], r_r.at[0, u], oy))

    def step2(u):
        i, m = units[u]
        q, sm = qs[i], side[m]
        one[u].wait_recv()
        if i == 0:
            dw[q, :, x, c, :, sm] = dw[q, :, x, c, :, sm] + r1[u]
            two[u] = go(_send(dw.at[q, 1 - y, x, c, :, sm], r2.at[u], r_s.at[1, u], r_r.at[1, u], oy))
        else:
            dw[q, y, :, c, :, sm] = dw[q, y, :, c, :, sm] + r1[u]
            two[u] = go(_send(dw.at[q, y, 1 - x, c, :, sm], r2.at[u], r_s.at[1, u], r_r.at[1, u], ox))

    def step3(u):
        i, m = units[u]
        q, sm = qs[i], side[m]
        two[u].wait_recv()
        dw[q, y, x, c, :, sm] = dw[q, y, x, c, :, sm] + r2[u]
        if i == 0:
            three[m] = go(_send(dw.at[q, y, x, c, :, sm], rz.at[m], r_s.at[2, u], r_r.at[2, u], ozl))

    e1.wait_recv()
    cores = [own_grad(0), own_grad(1)]
    k3.wait_recv()
    sb[:, y, x] = sb[:, y, x] + s3[...]
    k4 = [go(_send(sb.at[zs[i], y, x], s4.at[i], t_s.at[i], t_r.at[i], oz[i])) for i in range(3)]
    step1(0)
    step1(1)
    e2.wait_recv()
    cores += [own_grad(2), own_grad(3)]
    step2(0)
    step2(1)
    step1(2)
    step1(3)
    for cp in k4:
        cp.wait_recv()
    g[z, y, x, c] = ((sb[z, y, x] + s4[0]) + s4[1]) + s4[2]
    k5 = [go(_send(g.at[z, y, x, c], g.at[z, y, x, c], u_s.at[i], u_r.at[i], oz[i])) for i in range(3)]
    step3(0)
    step3(1)
    for cp in k5:
        cp.wait_recv()
    k6 = small(3, g.at[:, y, x, c], g.at[:, y, x, c], oy)
    step2(2)
    k6.wait_recv()
    k7 = small(4, g.at[:, :, x, c], g.at[:, :, x, c], ox)
    step2(3)
    k7.wait_recv()
    k8 = small(5, g.at[:, :, :, c], g.at[:, :, :, c], oc)
    step3(2)
    k8.wait_recv()
    for t in range(n):
        cbi, r, _ = place(t)
        v = g[t // 8, (t // 4) % 2, (t // 2) % 2, t % 2]
        o = o2s if cbi < 2 else o2n
        o[pl.ds(r * h2r, h2r), pl.ds((cbi % 2) * 128, 128)] = v[:h2r]
        d3w[pl.ds(r * h3r, h3r), pl.ds(cbi * 128, 128)] = v[h2r:]
    oloss[...] = d3w[48:56, :128]
    o3s[...] = d3w[:classes, left]
    o3n[...] = d3w[:classes, right]
    step3(3)
    three[0].wait_recv()
    o1s[...] = dw[zl, y, x, c, :, left] + rz[0]
    three[1].wait_recv()
    o1n[...] = dw[zl, y, x, c, :, right] + rz[1]

    for e, b in enumerate(bufs):
        hdrain(b, e)
    gdn, gup = gcopies()

    @pl.when(has_lo)
    def _():
        gdn.wait_send()

    @pl.when(has_hi)
    def _():
        gup.wait_send()

    for s in range(3):
        def drain(k, _):
            xcopy(s, k).wait_send()
            return 0

        lax.fori_loop(1, 16, drain, 0)
    for cp in done:
        cp.wait_send()


def _pass(*refs):
    k = len(refs) // 2
    for i, o in zip(refs[:k], refs[k:]):
        o[...] = i[:o.shape[0], :o.shape[1]]


def solution(mesh):
    n = mesh.shape['g']
    vm = pl.BlockSpec(memory_space=pltpu.VMEM)
    hbm = pl.BlockSpec(memory_space=pl.ANY)
    dma = pltpu.SemaphoreType.DMA
    sds = jax.ShapeDtypeStruct

    def body(x, ws1, wn1, ws2, wn2, ws3, wn3, nbr, nmask, labels):
        nodes = x.shape[0]
        rows, slots = nbr.shape
        fd, hid = ws1.shape
        classes = ws3.shape[1]
        per = hid // 8 + 8
        w = 2 * hid
        v = pltpu.VMEM
        scratch = [
            v((2 * rows, 16 * fd), BF), v((2, 2, 2, 2, fd, w), BF), v((rows, w), F32), v((rows, w), F32),
            v((3 * rows, hid), F32), v((rows, 3 * rows), BF), v((rows, 3 * rows), BF), v((3 * rows, 128), BF),
            v((3, 8, rows), I32), v((128, hid), BF), v((128, hid), BF),
            v((3 * rows, hid), BF), v((3 * rows, hid), BF), v((3 * rows, 128), BF), v((3 * rows, hid), BF),
            v((3 * rows, hid), BF), v((2 * rows, w), BF),
            v((2, 2, 2, 2, fd, w), F32), v((2, 2, 2, fd, w), F32), v((4, 2, fd, hid), F32),
            v((4, fd, hid), F32), v((2, fd, hid), F32), v((hid, w), F32), v((128, w), F32), v((16, rows), F32),
            v((4, 2, 2, 2, per, 128), F32), v((4, 2, 2, per, 128), F32), v((4, 2, 2, per, 128), F32),
            v((4, 2, per, 128), F32), v((4, per, 128), F32), v((3, per, 128), F32), v((4, 2, 2, 2, per, 128), F32),
            dma((2,)), dma((3, 16)), dma((3, 16)), dma((10,)), dma((10,)), dma((4,)), dma((4,)), dma((8, 2)), dma((8, 2)),
            dma((2,)), dma((2,)), dma((4,)), dma((4,)), dma((3, 4)), dma((3, 4)), dma((6,)), dma((6,)),
            dma((3,)), dma((3,)), dma((3,)), dma((3,))]
        o1s, o1n, o2s, o2n, o3s, o3n, loss = pl.pallas_call(
            lambda *r: _step(n, classes, nodes, *r),
            out_shape=(sds((fd, hid), F32), sds((fd, hid), F32), sds((hid, hid), F32), sds((hid, hid), F32),
                       sds((classes, hid), F32), sds((classes, hid), F32), sds((8, 128), F32)),
            in_specs=[hbm] + [vm] * 9, out_specs=(vm,) * 7, scratch_shapes=scratch,
            compiler_params=pltpu.CompilerParams(collective_id=0, has_side_effects=True, vmem_limit_bytes=60 << 20),
            name='step',
        )(x, ws1, wn1, ws2, wn2, ws3.T, wn3.T, nbr.T, nmask.T, labels[None])
        outs = (o1s, o1n, o2s, o2n, o3s, o3n, loss)
        outs = pl.pallas_call(
            _pass, out_shape=tuple(sds(o.shape, F32) for o in outs[:6]) + (sds((1, 1), F32),), in_specs=[vm] * 7, out_specs=(vm,) * 7,
            name='pass_on')(*outs)
        o1s, o1n, o2s, o2n, o3s, o3n, loss = outs
        return loss[0, 0], o1s, o1n, o2s, o2n, o3s.T, o3n.T

    r = P('g', None)
    in_specs = (P(None, 'g'), r, r, P(), P(), P(), P(), r, r, P('g'))
    out_specs = (P(), r, r, P(), P(), P(), P())
    return jax.shard_map(body, mesh=mesh, in_specs=in_specs, out_specs=out_specs, check_vma=False)
```

time: 221 us -> 186 us (0.84)
  local copies, waits for them, and re-layouts: 18.6 us -> 0 us
  Pallas kernels: 198 us -> 184 us
    pallas_call x1, Pallas kernels: 198 us -> 182 us  [body(): pl.pallas_call(lambda *r: _step(n, classes, nodes, *r), out_shape=(sds((f...]
    unnamed x10 -> x0, local copies, waits for them, and re-layouts: 15.9 us -> none
where the time goes in v3:
time: 186 us; the launch traced here: 184 us
  Pallas kernels  184 us (99%)
    pallas_call x1, Pallas kernels, body(): pl.pallas_call(lambda *r: _step(n, classes, nodes, *r), out_shape=(sds((f...  182 us

profile of v3, /device:TPU:0, one launch (start us, length us, event | category | flops | bytes accessed | tf_op | source)
XLA Modules:
  0.0 184.3 jit_solution(6069534507969527558)
XLA Ops:
  0.6 181.6 %step.1 = (f32[128,256]{1,0:T(8,128)}, f32[128,256]{1,0:T(8,128)}, f32[256,256]{1,0:T(8,128)}, f32[256,256]{1,0:T(8,128)}, f32[47,256]{1,0:T(8,128)}, /*index=5*/f32[47,256]{1,0:T(8,128)}, f32[8,128]{1,0:T(8,128)}) custom-call(bf16[16384,128]{1,0:T(8,128)(2,1)} %r_0_.1, bf16[128,256]{1,0:T(8,128)(2,1)} %r_1_.1, bf16[128,256]{1,0:T(8,128)(2,1)} %r_2_.1, ...), custom_call_target="tpu_custom_call" | custom-call | tf_op jit(solution)/shard_map/step/pallas_call | solution.py:524
  182.2 2.1 %pass_on.1 = (f32[128,256]{1,0:T(8,128)}, f32[128,256]{1,0:T(8,128)}, f32[256,256]{1,0:T(8,128)}, f32[256,256]{1,0:T(8,128)}, f32[47,256]{1,0:T(8,128)}, /*index=5*/f32[47,256]{1,0:T(8,128)}, f32[1,1]{1,0:T(1,128)}) custom-call(f32[128,256]{1,0:T(8,128)} %get-tuple-element.21.refs_0_, f32[128,256]{1,0:T(8,128)} %get-tuple-element.22.refs_1_, ...), custom_call_target="tpu_custom_call" | custom-call | tf_op jit(solution)/shard_map/pass_on/pallas_call | solution.py:533

commit v4 on v3

--- a/solution.py
+++ b/solution.py
@@ -44,9 +44,9 @@
 def _step(n, classes, nodes,
           xh, ws1, wn1, ws2, wn2, ws3, wn3, nbr, nmask, lab,
           o1s, o1n, o2s, o2n, o3s, o3n, oloss,
-          xb, wb, pp, pr, nx, a, bt, cx, gx, w3, w3n, h1x, h2x, d3x, d2x, d1x, dbx,
+          xb, wb, pp, pr, nn, a, ap, bt, cx, gx, gp, w3, w3n, h1x, h2x, d3x, d2x, d1x, dbx,
           dw, rc, r1, r2, rz, d2w, d3w, gt, sa, sb, s1, s2, s3, s4, g,
-          xl, xs_s, xs_r, w_s, w_r, p_s, p_r, h_s, h_r, e_s, e_r, c_s, c_r, r_s, r_r, q_s, q_r, t_s, t_r, u_s, u_r):
+          xl, xs_s, xs_r, w_s, w_r, p_s, p_r, n_s, n_r, h_s, h_r, e_s, e_r, c_s, c_r, r_s, r_r, q_s, q_r, t_s, t_r, u_s, u_r):
     slots, rows = nbr.shape
     hid = ws2.shape[0]
     fd = ws1.shape[0]
@@ -89,17 +89,13 @@
     wb[zl, y, x, c, :, right] = wn1[...]
     pl.semaphore_wait(bar, n - 1)
 
-    part = rows // 2
-
     def xcopy(s, k):
         t = first + jnp.bitwise_xor(j, k)
-        if s < 2:
-            r = (t + 16 - 32 * zh) * rows + s * part
-            to = pl.ds(rows + s * part, part)
-            size = part
-        else:
-            r, to, size = t * rows, top, rows
-        return _send(xh.at[pl.ds(pl.multiple_of(r, part), size)], xb.at[to, mycol], xs_s.at[s, k], xs_r.at[s, k], t)
+        src, to = (xrows(t + 16 - 32 * zh), bot) if s == 0 else (xrows(t), top)
+        return _send(src, xb.at[to, mycol], xs_s.at[s, k], xs_r.at[s, k], t)
+
+    seam = (me == n // 2 - 1) | (me == n // 2)
+    ks = jnp.bitwise_xor(j, jnp.where(zh == 0, 15, 0))
 
     order = (1, 2, 4, 8, 3, 5, 9, 14, 15, 6, 10, 12, 7, 11, 13)
 
@@ -161,21 +157,69 @@
         def _():
             up.wait_send()
 
+    has = [(me > 0, me < n - 1), (partner > 0, partner < n - 1)]
+
+    def ncopies(s):
+        dn = _send(nn.at[s, own], nn.at[jnp.where(j > 0, s, 1 - s), hi], n_s.at[s, 0],
+                   n_r.at[jnp.where(j > 0, s, 1 - s), 0], jnp.where(j > 0, me - 1, first + 15))
+        up = _send(nn.at[s, own], nn.at[jnp.where(j < 15, s, 1 - s), lo], n_s.at[s, 1],
+                   n_r.at[jnp.where(j < 15, s, 1 - s), 1], jnp.where(j < 15, me + 1, first))
+        return dn, up
+
+    def nstart(s):
+        dn, up = ncopies(s)
+
+        @pl.when(has[s][0])
+        def _():
+            dn.start()
+
+        @pl.when(has[s][1])
+        def _():
+            up.start()
+
+    def narrive(s):
+        @pl.when(has[s][1])
+        def _():
+            _send(nn.at[s, own], nn.at[s, hi], n_s.at[s, 0], n_r.at[s, 0], partner).wait_recv()
+
+        @pl.when(has[s][0])
+        def _():
+            _send(nn.at[s, own], nn.at[s, lo], n_s.at[s, 1], n_r.at[s, 1], partner).wait_recv()
+
+    def ndrain(s):
+        dn, up = ncopies(s)
+
+        @pl.when(has[s][0])
+        def _():
+            dn.wait_send()
+
+        @pl.when(has[s][1])
+        def _():
+            up.wait_send()
+
     def gcopies():
         return (_send(gx.at[1], gx.at[2], h_s.at[7, 0], h_r.at[7, 0], me - 1),
                 _send(gx.at[1], gx.at[0], h_s.at[7, 1], h_r.at[7, 1], me + 1))
 
-    bufs = (nx, h1x, h2x, d3x, d2x, d1x, cx)
+    bufs = {1: h1x, 2: h2x, 3: d3x, 4: d2x, 5: d1x, 6: cx}
+    for s in range(2):
+        @pl.when(jnp.logical_not(has[s][0]))
+        def _():
+            nn[s, lo] = jnp.ones((rows, hid), F32)
+
+        @pl.when(jnp.logical_not(has[s][1]))
+        def _():
+            nn[s, hi] = jnp.ones((rows, hid), F32)
 
     @pl.when(jnp.logical_not(has_lo))
     def _():
-        for b in bufs:
+        for b in bufs.values():
             b[lo] = jnp.ones((rows, b.shape[1]), b.dtype)
         gx[0] = jnp.full(gx.shape[1:], -1, I32)
 
     @pl.when(jnp.logical_not(has_hi))
     def _():
-        for b in bufs:
+        for b in bufs.values():
             b[hi] = jnp.ones((rows, b.shape[1]), b.dtype)
         gx[2] = jnp.full(gx.shape[1:], -1, I32)
 
@@ -195,6 +239,7 @@
     gt[slots:slots + 1] = jnp.where(trem > 0, trem - 1 - base + rows, -1).astype(F32)
     gt[slots + 1:slots + 2] = tc.astype(F32)
     gt[slots + 2:slots + 3] = lab[...].astype(F32)
+    kg = go(_send(gt, gp, e_s.at[2], e_r.at[2], partner))
     gc = gt[...].T
     cnt = gc[:, slots + 1:slots + 2]
     labc = gc[:, slots + 2:slots + 3].astype(I32)
@@ -217,14 +262,32 @@
         f.wait_recv()
     fr = wsend(7, wb.at[:, y, :, c, :, right], oy)
     xgo(0, order[7:])
-    lin = gc[:, 0:slots].astype(I32)
-    rem = gc[:, slots:slots + 1].astype(I32)
     col = lax.broadcasted_iota(I32, (rows, rows), 1)
-    acc = jnp.zeros((rows, rows), F32)
-    for k in range(slots):
-        acc = acc + (lin[:, k:k + 1] == col).astype(F32)
-    a[:, own] = acc.astype(BF)
-    xgo(1, order)
+
+    def counts(dst, v):
+        lin = v[:, 0:slots].astype(I32)
+        rem = v[:, slots:slots + 1].astype(I32)
+        acc = jnp.zeros((rows, rows), F32)
+        for k in range(slots):
+            acc = acc + (lin[:, k:k + 1] == col).astype(F32)
+        dst[:, own] = acc.astype(BF)
+        dst[:, lo] = (rem == col).astype(F32).astype(BF)
+        dst[:, hi] = (rem == col + 2 * rows).astype(F32).astype(BF)
+
+
+    @pl.when(jnp.logical_not(seam))
+    def _():
+        xcopy(1, ks).start()
+
+    for k in order:
+        @pl.when(ks != k)
+        def _():
+            xcopy(1, k).start()
+
+    kg.wait_recv()
+    gq = gp[...].T
+    counts(ap, gq)
+    cntp = gq[:, slots + 1:slots + 2]
     row = lax.broadcasted_iota(I32, (rows, rows), 0)
     acc = jnp.zeros((rows, rows), F32)
     for k in range(slots):
@@ -234,27 +297,26 @@
     fr = wsend(8, wb.at[:, :, :, c, :, right], oc)
     fl.wait_recv()
     fl = wsend(9, wb.at[:, :, :, c, :, left], oc)
+    counts(a, gc)
     keep[0].wait()
     xarrive(0)
-    xgo(2, order)
 
     fr.wait_recv()
     fl.wait_recv()
-    p1, p2 = pl.ds(0, part), pl.ds(part, part)
-    f1, f2 = pl.ds(rows, part), pl.ds(rows + part, part)
 
     def wcols(cols):
         return wb[:, :, :, :, :, cols].reshape(16 * fd, hid)
 
-    def swap(i, rs, cols):
-        return go(_send(pp.at[rs, cols], pr.at[rs, cols], p_s.at[i], p_r.at[i], partner))
-
-    pp[p1, right] = _dot(xb[f1], wcols(right))
-    cn1 = swap(0, p1, right)
-    pp[p1, left] = _dot(xb[f1], wcols(left))
-    cs1 = swap(2, p1, left)
-    a[:, lo] = (rem == col).astype(F32).astype(BF)
-    a[:, hi] = (rem == col + 2 * rows).astype(F32).astype(BF)
+    def near(m, s):
+        return _sum3(_dot(m[:, own], _split3(nn[s, own])))
+
+    def far(m, s):
+        return _sum3(_dot(m[:, lo], _split3(nn[s, lo]))) + _sum3(_dot(m[:, hi], _split3(nn[s, hi])))
+
+    nn[1, own] = _dot(xb[bot], wcols(right))
+    nstart(1)
+    zp = _dot(xb[bot], wcols(left))
+    accp = near(ap, 1)
     gdn, gup = gcopies()
 
     @pl.when(has_hi)
@@ -276,26 +338,31 @@
     def back(at, v):
         return _sum3(_dot(bt[:, at], _split3(v / cx[at, 0:1].astype(F32))))
 
-    xarrive(1)
-    pp[p2, right] = _dot(xb[f2], wcols(right))
-    cn2 = swap(1, p2, right)
-    pp[p2, left] = _dot(xb[f2], wcols(left))
-    cs2 = swap(3, p2, left)
+    def begin():
+        xarrive(1)
+        nn[0, own] = _dot(xb[top], wcols(right))
+        nstart(0)
+
     keep[1].wait()
-    xarrive(2)
-    po = _dot(xb[top], wcols(right))
-    cn1.wait_recv()
-    cn2.wait_recv()
-    nx[own] = po + pr[:, right]
-    hstart(nx, 0)
-    po = _dot(xb[top], wcols(left))
-    acc = _sum3(_dot(a[:, own], _split3(nx[own])))
-    harrive(nx, 0)
-    acc = acc + _sum3(_dot(a[:, lo], _split3(nx[lo]))) + _sum3(_dot(a[:, hi], _split3(nx[hi])))
-    acc = po + acc / cnt
-    cs1.wait_recv()
-    cs2.wait_recv()
-    z1 = acc + pr[:, left]
+
+    @pl.when(seam)
+    def _():
+        begin()
+
+    narrive(1)
+    pp[...] = zp + (accp + far(ap, 1)) / cntp
+    cs = go(_send(pp, pr, p_s.at[0], p_r.at[0], partner))
+
+    @pl.when(jnp.logical_not(seam))
+    def _():
+        begin()
+
+    z1 = _dot(xb[top], wcols(left))
+    acc = near(a, 0)
+    narrive(0)
+    z1 = z1 + (acc + far(a, 0)) / cnt
+    cs.wait_recv()
+    z1 = z1 + pr[...]
     h1 = jnp.maximum(z1, 0.0).astype(BF)
     h1x[own] = h1
     hstart(h1x, 1)
@@ -361,7 +428,21 @@
     hstart(d1x, 5)
     dbx[top, left] = d1
     e1 = go(_send(dbx.at[top, left], dbx.at[bot, left], e_s.at[0], e_r.at[0], partner))
+    qs = [1 - zl, zl]
+    wide = 8 * fd
+    units = [(i, m) for m in range(2) for i in range(2)]
+    side = [left, right]
+
+    def feats(q):
+        return pl.ds(pl.multiple_of(q * wide, wide), wide)
+
+    def own_grad(m):
+        for q in qs:
+            v = _tdot(xb[top, feats(q)], dbx[top, side[m]])
+            dw[q, :, :, :, :, side[m]] = v.reshape(2, 2, 2, fd, hid)
+
     b1 = back(own, d1.astype(F32))
+    own_grad(0)
     k1.wait_recv()
     sb[...] = sa[:, :, :, c] + s1[...]
     k2 = small(1, sb.at[:, :, 1 - x], s2, ox)
@@ -373,20 +454,11 @@
     sb[:, :, x] = sb[:, :, x] + s2[...]
     k3 = small(2, sb.at[:, 1 - y, x], s3, oy)
 
-    qs = [1 - zl, zl]
-    wide = 8 * fd
-
-    def feats(q):
-        return pl.ds(pl.multiple_of(q * wide, wide), wide)
-
-    units = [(i, m) for m in range(2) for i in range(2)]
-    side = [left, right]
-
-    def own_grad(u):
+    def partner_grad(u):
         i, m = units[u]
         q = qs[i]
-        v = _tdot(xb[:, feats(q)], dbx[:, side[m]])
-        dw[q, :, :, :, :, side[m]] = v.reshape(2, 2, 2, fd, hid)
+        v = _tdot(xb[bot, feats(q)], dbx[bot, side[m]]).reshape(2, 2, 2, fd, hid)
+        dw[q, :, :, :, :, side[m]] = dw[q, :, :, :, :, side[m]] + v
         return go(_send(dw.at[q, :, :, 1 - c, :, side[m]], rc.at[q, :, :, :, side[m]], c_s.at[u], c_r.at[u], oc))
 
     one, two, three = {}, {}, {}
@@ -420,15 +492,16 @@
         if i == 0:
             three[m] = go(_send(dw.at[q, y, x, c, :, sm], rz.at[m], r_s.at[2, u], r_r.at[2, u], ozl))
 
+    own_grad(1)
     e1.wait_recv()
-    cores = [own_grad(0), own_grad(1)]
+    cores = [partner_grad(0), partner_grad(1)]
     k3.wait_recv()
     sb[:, y, x] = sb[:, y, x] + s3[...]
     k4 = [go(_send(sb.at[zs[i], y, x], s4.at[i], t_s.at[i], t_r.at[i], oz[i])) for i in range(3)]
     step1(0)
     step1(1)
     e2.wait_recv()
-    cores += [own_grad(2), own_grad(3)]
+    cores += [partner_grad(2), partner_grad(3)]
     step2(0)
     step2(1)
     step1(2)
@@ -465,8 +538,10 @@
     three[1].wait_recv()
     o1n[...] = dw[zl, y, x, c, :, right] + rz[1]
 
-    for e, b in enumerate(bufs):
+    for e, b in bufs.items():
         hdrain(b, e)
+    ndrain(0)
+    ndrain(1)
     gdn, gup = gcopies()
 
     @pl.when(has_lo)
@@ -477,7 +552,7 @@
     def _():
         gup.wait_send()
 
-    for s in range(3):
+    for s in range(2):
         def drain(k, _):
             xcopy(s, k).wait_send()
             return 0
@@ -509,17 +584,17 @@
         w = 2 * hid
         v = pltpu.VMEM
         scratch = [
-            v((2 * rows, 16 * fd), BF), v((2, 2, 2, 2, fd, w), BF), v((rows, w), F32), v((rows, w), F32),
-            v((3 * rows, hid), F32), v((rows, 3 * rows), BF), v((rows, 3 * rows), BF), v((3 * rows, 128), BF),
-            v((3, 8, rows), I32), v((128, hid), BF), v((128, hid), BF),
+            v((2 * rows, 16 * fd), BF), v((2, 2, 2, 2, fd, w), BF), v((rows, hid), F32), v((rows, hid), F32),
+            v((2, 3 * rows, hid), F32), v((rows, 3 * rows), BF), v((rows, 3 * rows), BF), v((rows, 3 * rows), BF),
+            v((3 * rows, 128), BF), v((3, 8, rows), I32), v((16, rows), F32), v((128, hid), BF), v((128, hid), BF),
             v((3 * rows, hid), BF), v((3 * rows, hid), BF), v((3 * rows, 128), BF), v((3 * rows, hid), BF),
             v((3 * rows, hid), BF), v((2 * rows, w), BF),
             v((2, 2, 2, 2, fd, w), F32), v((2, 2, 2, fd, w), F32), v((4, 2, fd, hid), F32),
             v((4, fd, hid), F32), v((2, fd, hid), F32), v((hid, w), F32), v((128, w), F32), v((16, rows), F32),
             v((4, 2, 2, 2, per, 128), F32), v((4, 2, 2, per, 128), F32), v((4, 2, 2, per, 128), F32),
             v((4, 2, per, 128), F32), v((4, per, 128), F32), v((3, per, 128), F32), v((4, 2, 2, 2, per, 128), F32),
-            dma((2,)), dma((3, 16)), dma((3, 16)), dma((10,)), dma((10,)), dma((4,)), dma((4,)), dma((8, 2)), dma((8, 2)),
-            dma((2,)), dma((2,)), dma((4,)), dma((4,)), dma((3, 4)), dma((3, 4)), dma((6,)), dma((6,)),
+            dma((2,)), dma((2, 16)), dma((2, 16)), dma((10,)), dma((10,)), dma((1,)), dma((1,)), dma((2, 2)), dma((2, 2)),
+            dma((8, 2)), dma((8, 2)), dma((3,)), dma((3,)), dma((4,)), dma((4,)), dma((3, 4)), dma((3, 4)), dma((6,)), dma((6,)),
             dma((3,)), dma((3,)), dma((3,)), dma((3,))]
         o1s, o1n, o2s, o2n, o3s, o3n, loss = pl.pallas_call(
             lambda *r: _step(n, classes, nodes, *r),

time: 186 us -> 179 us (0.962)
  Pallas kernels: 184 us -> 177 us
    pallas_call x1, Pallas kernels: 182 us -> 175 us  [body(): pl.pallas_call(lambda *r: _step(n, classes, nodes, *r), out_shape=(sds((f...]
where the time goes in v4:
time: 179 us; the launch traced here: 178 us
  Pallas kernels  177 us (99%)
    pallas_call x1, Pallas kernels, body(): pl.pallas_call(lambda *r: _step(n, classes, nodes, *r), out_shape=(sds((f...  175 us

profile of v4, /device:TPU:0, one launch (start us, length us, event | category | flops | bytes accessed | tf_op | source)
XLA Modules:
  0.0 178.1 jit_solution(520791224563910659)
XLA Ops:
  0.6 175.4 %step.1 = (f32[128,256]{1,0:T(8,128)}, f32[128,256]{1,0:T(8,128)}, f32[256,256]{1,0:T(8,128)}, f32[256,256]{1,0:T(8,128)}, f32[47,256]{1,0:T(8,128)}, /*index=5*/f32[47,256]{1,0:T(8,128)}, f32[8,128]{1,0:T(8,128)}) custom-call(bf16[16384,128]{1,0:T(8,128)(2,1)} %r_0_.1, bf16[128,256]{1,0:T(8,128)(2,1)} %r_1_.1, bf16[128,256]{1,0:T(8,128)(2,1)} %r_2_.1, ...), custom_call_target="tpu_custom_call" | custom-call | tf_op jit(solution)/shard_map/step/pallas_call | solution.py:599
  176.0 2.1 %pass_on.1 = (f32[128,256]{1,0:T(8,128)}, f32[128,256]{1,0:T(8,128)}, f32[256,256]{1,0:T(8,128)}, f32[256,256]{1,0:T(8,128)}, f32[47,256]{1,0:T(8,128)}, /*index=5*/f32[47,256]{1,0:T(8,128)}, f32[1,1]{1,0:T(1,128)}) custom-call(f32[128,256]{1,0:T(8,128)} %get-tuple-element.21.refs_0_, f32[128,256]{1,0:T(8,128)} %get-tuple-element.22.refs_1_, ...), custom_call_target="tpu_custom_call" | custom-call | tf_op jit(solution)/shard_map/pass_on/pallas_call | solution.py:608

commit v5 on v4

--- a/solution.py
+++ b/solution.py
@@ -69,13 +69,24 @@
         done.append(cp)
         return cp
 
+    seam = (me == n // 2 - 1) | (me == n // 2)
     bar = pltpu.get_barrier_semaphore()
 
-    def greet(k, _):
-        pl.semaphore_signal(bar, inc=1, device_id=(lax.rem(me + k, n),), device_id_type=MESH)
+    def greet(t):
+        pl.semaphore_signal(bar, inc=1, device_id=(t,), device_id_type=MESH)
+
+    greet(partner)
+    greet(partner + 8 - 16 * zl)
+
+    @pl.when(seam)
+    def _():
+        greet(jnp.where(me == n // 2 - 1, me + 1, me - 1))
+
+    def greet_half(k, _):
+        greet(first + jnp.bitwise_xor(j, k))
         return 0
 
-    lax.fori_loop(1, n, greet, 0)
+    lax.fori_loop(1, 16, greet_half, 0)
 
     def xrows(t):
         return xh.at[pl.ds(pl.multiple_of(t * rows, rows), rows)]
@@ -87,17 +98,16 @@
         cp.start()
     wb[zl, y, x, c, :, left] = ws1[...]
     wb[zl, y, x, c, :, right] = wn1[...]
-    pl.semaphore_wait(bar, n - 1)
+    pl.semaphore_wait(bar, 17 + seam.astype(I32))
 
     def xcopy(s, k):
         t = first + jnp.bitwise_xor(j, k)
         src, to = (xrows(t + 16 - 32 * zh), bot) if s == 0 else (xrows(t), top)
         return _send(src, xb.at[to, mycol], xs_s.at[s, k], xs_r.at[s, k], t)
 
-    seam = (me == n // 2 - 1) | (me == n // 2)
     ks = jnp.bitwise_xor(j, jnp.where(zh == 0, 15, 0))
 
-    order = (1, 2, 4, 8, 3, 5, 9, 14, 15, 6, 10, 12, 7, 11, 13)
+    order = (14, 15, 6, 10, 12, 7, 11, 13, 2, 4, 8, 3, 5, 9, 1)
 
     def xgo(s, ks):
         for k in ks:
@@ -350,8 +360,15 @@
         begin()
 
     narrive(1)
-    pp[...] = zp + (accp + far(ap, 1)) / cntp
-    cs = go(_send(pp, pr, p_s.at[0], p_r.at[0], partner))
+    fl, fh = _split3(nn[1, lo]), _split3(nn[1, hi])
+    part = rows // 2
+    cs = []
+    for i in range(2):
+        r = slice(i * part, (i + 1) * part)
+        v = _sum3(_dot(ap[r, lo], fl)) + _sum3(_dot(ap[r, hi], fh))
+        pp[r] = zp[r] + (accp[r] + v) / cntp[r]
+        at = pl.ds(i * part, part)
+        cs.append(go(_send(pp.at[at], pr.at[at], p_s.at[i], p_r.at[i], partner)))
 
     @pl.when(jnp.logical_not(seam))
     def _():
@@ -361,7 +378,8 @@
     acc = near(a, 0)
     narrive(0)
     z1 = z1 + (acc + far(a, 0)) / cnt
-    cs.wait_recv()
+    for cp in cs:
+        cp.wait_recv()
     z1 = z1 + pr[...]
     h1 = jnp.maximum(z1, 0.0).astype(BF)
     h1x[own] = h1
@@ -583,19 +601,20 @@
         per = hid // 8 + 8
         w = 2 * hid
         v = pltpu.VMEM
+        cube, box, tile = (2, 2, 2), (4, 2, 2), (per, 128)
+        ext = v((3 * rows, hid), BF)
         scratch = [
-            v((2 * rows, 16 * fd), BF), v((2, 2, 2, 2, fd, w), BF), v((rows, hid), F32), v((rows, hid), F32),
+            v((2 * rows, 16 * fd), BF), v(cube + (2, fd, w), BF), v((rows, hid), F32), v((rows, hid), F32),
             v((2, 3 * rows, hid), F32), v((rows, 3 * rows), BF), v((rows, 3 * rows), BF), v((rows, 3 * rows), BF),
             v((3 * rows, 128), BF), v((3, 8, rows), I32), v((16, rows), F32), v((128, hid), BF), v((128, hid), BF),
-            v((3 * rows, hid), BF), v((3 * rows, hid), BF), v((3 * rows, 128), BF), v((3 * rows, hid), BF),
-            v((3 * rows, hid), BF), v((2 * rows, w), BF),
-            v((2, 2, 2, 2, fd, w), F32), v((2, 2, 2, fd, w), F32), v((4, 2, fd, hid), F32),
+            ext, ext, v((3 * rows, 128), BF), ext, ext, v((2 * rows, w), BF),
+            v(cube + (2, fd, w), F32), v(cube + (fd, w), F32), v((4, 2, fd, hid), F32),
             v((4, fd, hid), F32), v((2, fd, hid), F32), v((hid, w), F32), v((128, w), F32), v((16, rows), F32),
-            v((4, 2, 2, 2, per, 128), F32), v((4, 2, 2, per, 128), F32), v((4, 2, 2, per, 128), F32),
-            v((4, 2, per, 128), F32), v((4, per, 128), F32), v((3, per, 128), F32), v((4, 2, 2, 2, per, 128), F32),
-            dma((2,)), dma((2, 16)), dma((2, 16)), dma((10,)), dma((10,)), dma((1,)), dma((1,)), dma((2, 2)), dma((2, 2)),
-            dma((8, 2)), dma((8, 2)), dma((3,)), dma((3,)), dma((4,)), dma((4,)), dma((3, 4)), dma((3, 4)), dma((6,)), dma((6,)),
-            dma((3,)), dma((3,)), dma((3,)), dma((3,))]
+            v(box + (2,) + tile, F32), v(box + tile, F32), v(box + tile, F32),
+            v((4, 2) + tile, F32), v((4,) + tile, F32), v((3,) + tile, F32), v(box + (2,) + tile, F32),
+            dma((2,))]
+        for d in ((2, 16), (10,), (2,), (2, 2), (8, 2), (3,), (4,), (3, 4), (6,), (3,), (3,)):
+            scratch += [dma(d), dma(d)]
         o1s, o1n, o2s, o2n, o3s, o3n, loss = pl.pallas_call(
             lambda *r: _step(n, classes, nodes, *r),
             out_shape=(sds((fd, hid), F32), sds((fd, hid), F32), sds((hid, hid), F32), sds((hid, hid), F32),

time: 179 us -> 176 us (0.983)
  Pallas kernels: 177 us -> 174 us
    pallas_call x1, Pallas kernels: 175 us -> 172 us  [body(): pl.pallas_call(lambda *r: _step(n, classes, nodes, *r), out_shape=(sds((f...]
where the time goes in v5:
time: 176 us; the launch traced here: 175 us
  Pallas kernels  174 us (99%)
    pallas_call x1, Pallas kernels, body(): pl.pallas_call(lambda *r: _step(n, classes, nodes, *r), out_shape=(sds((f...  172 us

profile of v5, /device:TPU:0, one launch (start us, length us, event | category | flops | bytes accessed | tf_op | source)
XLA Modules:
  0.0 174.9 jit_solution(10751580776665813475)
XLA Ops:
  0.6 172.2 %step.1 = (f32[128,256]{1,0:T(8,128)}, f32[128,256]{1,0:T(8,128)}, f32[256,256]{1,0:T(8,128)}, f32[256,256]{1,0:T(8,128)}, f32[47,256]{1,0:T(8,128)}, /*index=5*/f32[47,256]{1,0:T(8,128)}, f32[8,128]{1,0:T(8,128)}) custom-call(bf16[16384,128]{1,0:T(8,128)(2,1)} %r_0_.1, bf16[128,256]{1,0:T(8,128)(2,1)} %r_1_.1, bf16[128,256]{1,0:T(8,128)(2,1)} %r_2_.1, ...), custom_call_target="tpu_custom_call" | custom-call | tf_op jit(solution)/shard_map/step/pallas_call | solution.py:618
  172.8 2.1 %pass_on.1 = (f32[128,256]{1,0:T(8,128)}, f32[128,256]{1,0:T(8,128)}, f32[256,256]{1,0:T(8,128)}, f32[256,256]{1,0:T(8,128)}, f32[47,256]{1,0:T(8,128)}, /*index=5*/f32[47,256]{1,0:T(8,128)}, f32[1,1]{1,0:T(1,128)}) custom-call(f32[128,256]{1,0:T(8,128)} %get-tuple-element.21.refs_0_, f32[128,256]{1,0:T(8,128)} %get-tuple-element.22.refs_1_, ...), custom_call_target="tpu_custom_call" | custom-call | tf_op jit(solution)/shard_map/pass_on/pallas_call | solution.py:627
